TPU v7x, 32 devices: a whole 2x2x4 slice. The times are simulated.
32 devices in a mesh: dp: 2 (over x), cp: 4 (over z), tp: 4 (over y, core).
Axes of the slice: x: 2, y: 2, z: 4, core: 2. Of those that a mesh axis runs over, the one named last changes fastest.
Arguments:
- x: bfloat16 [2, 8192, 3072], P('dp', ('cp', 'tp')), parts along dimension 0
- g_attn: bfloat16 [3072], replicated
- w_q: bfloat16 [3072, 24, 128], P(None, 'tp')
- w_k: bfloat16 [3072, 8, 128], P(None, 'tp')
- w_v: bfloat16 [3072, 8, 128], P(None, 'tp')
- w_o: bfloat16 [24, 128, 3072], P('tp')
- g_mlp: bfloat16 [3072], replicated
- w_gate: bfloat16 [3072, 8192], P(None, 'tp')
- w_up: bfloat16 [3072, 8192], P(None, 'tp')
- w_down: bfloat16 [8192, 3072], P('tp')
Outputs:
- output: bfloat16 [2, 8192, 3072], P('dp', ('cp', 'tp')), parts along dimension 0
There are 2 independent parts. A program takes and returns all parts, laid end to end along the dimension named above; an argument that names none is the same for every part.
All inputs are finite; a program needn't handle non-finite values.
Results may differ from a plain program's by a relative error of at most 0.02.
Values are sent between devices in bfloat16 or wider.
A program may use at most 1 GiB of HBM per device.

v0:
```python
import jax
import jax.numpy as jnp
from jax import lax
from jax.sharding import PartitionSpec as P

NORM_EPS = 1e-5
ROPE_THETA = 500000.0
TILE_ROWS = 256


def rms_norm(rows_in, gain_vec):
    rows_f32 = rows_in.astype(jnp.float32)
    mean_sq = jnp.mean(rows_f32 * rows_f32, axis=-1, keepdims=True)
    return (rows_f32 * lax.rsqrt(mean_sq + NORM_EPS) * gain_vec.astype(jnp.float32)).astype(jnp.bfloat16)


def apply_rope(heads_in, positions):
    head_dim = heads_in.shape[-1]
    half_dim = head_dim // 2
    inv_freq = ROPE_THETA ** (-2.0 * jnp.arange(half_dim, dtype=jnp.float32) / head_dim)
    angles = positions.astype(jnp.float32)[:, None] * inv_freq[None, :]
    angles = jnp.concatenate([angles, angles], axis=-1)[:, None, :]
    heads_f32 = heads_in.astype(jnp.float32)
    rotated = jnp.concatenate([-heads_f32[..., half_dim:], heads_f32[..., :half_dim]], axis=-1)
    return (heads_f32 * jnp.cos(angles) + rotated * jnp.sin(angles)).astype(jnp.bfloat16)


def stored_positions(row_ids, piece_len, cp_size):
    owner_cp = row_ids // (2 * piece_len)
    within = row_ids % (2 * piece_len)
    return jnp.where(within < piece_len, owner_cp * piece_len + within,
                     (2 * cp_size - 1 - owner_cp) * piece_len + within - piece_len)


def attend(q_rows, q_pos, keys, values, key_pos):
    q_len, n_kv_heads, group_size, head_dim = q_rows.shape
    n_tiles = max(1, q_len // TILE_ROWS)
    tile_len = q_len // n_tiles
    score_scale = head_dim ** -0.5

    def one_tile(tile_idx):
        row_start = tile_idx * tile_len
        q_tile = lax.dynamic_slice_in_dim(q_rows, row_start, tile_len, axis=0)
        pos_tile = lax.dynamic_slice_in_dim(q_pos, row_start, tile_len, axis=0)
        scores = jnp.einsum('qgrd,kgd->gqrk', q_tile, keys, preferred_element_type=jnp.float32) * score_scale
        visible = pos_tile[:, None, None] >= key_pos[None, None, :]
        scores = jnp.where(visible, scores, -1e30)
        weights = jnp.exp(scores - jnp.max(scores, axis=-1, keepdims=True))
        row_sum = jnp.sum(weights, axis=-1, keepdims=True)
        mixed_vals = jnp.einsum('gqrk,kgd->gqrd', weights.astype(jnp.bfloat16), values, preferred_element_type=jnp.float32) / row_sum
        return jnp.transpose(mixed_vals, (1, 0, 2, 3)).astype(jnp.bfloat16)

    tiles = lax.map(one_tile, jnp.arange(n_tiles))
    return tiles.reshape(q_len, n_kv_heads * group_size, head_dim)


def solution(mesh):
    cp_size = mesh.shape['cp']
    row_spec = P('dp', ('cp', 'tp'), None)
    head_cols = P(None, 'tp', None)

    def local_layer(x, g_attn, w_q, w_k, w_v, w_o, g_mlp, w_gate, w_up, w_down):
        x_rows = x[0]
        n_kv_local = w_k.shape[1]
        head_dim = w_q.shape[2]
        group_size = w_q.shape[1] // n_kv_local
        cp_index = lax.axis_index('cp')
        normed = lax.all_gather(rms_norm(x_rows, g_attn), 'tp', axis=0, tiled=True)
        seq_local = normed.shape[0]
        piece_len = seq_local // 2
        positions = stored_positions(cp_index * seq_local + jnp.arange(seq_local, dtype=jnp.int32), piece_len, cp_size)
        q_all = apply_rope(jnp.einsum('sd,dhk->shk', normed, w_q, preferred_element_type=jnp.float32).astype(jnp.bfloat16), positions)
        k_all = apply_rope(jnp.einsum('sd,dhk->shk', normed, w_k, preferred_element_type=jnp.float32).astype(jnp.bfloat16), positions)
        v_all = jnp.einsum('sd,dhk->shk', normed, w_v, preferred_element_type=jnp.float32).astype(jnp.bfloat16)
        k_seq = lax.all_gather(k_all, 'cp', axis=0, tiled=False)
        v_seq = lax.all_gather(v_all, 'cp', axis=0, tiled=False)
        key_pos = stored_positions(jnp.arange(cp_size * seq_local, dtype=jnp.int32), piece_len, cp_size).reshape(cp_size, seq_local)
        first_keys = k_seq[:, :piece_len].reshape(cp_size * piece_len, n_kv_local, head_dim)
        first_vals = v_seq[:, :piece_len].reshape(cp_size * piece_len, n_kv_local, head_dim)
        first_pos = key_pos[:, :piece_len].reshape(cp_size * piece_len)
        q_grp = q_all.reshape(seq_local, n_kv_local, group_size, head_dim)
        attn_first = attend(q_grp[:piece_len], positions[:piece_len], first_keys, first_vals, first_pos)
        attn_second = attend(q_grp[piece_len:], positions[piece_len:],
                             k_seq.reshape(cp_size * seq_local, n_kv_local, head_dim),
                             v_seq.reshape(cp_size * seq_local, n_kv_local, head_dim),
                             key_pos.reshape(cp_size * seq_local))
        attn_out = jnp.concatenate([attn_first, attn_second], axis=0)
        attn_part = jnp.einsum('shk,hkd->sd', attn_out, w_o, preferred_element_type=jnp.float32).astype(jnp.bfloat16)
        attn_rows = lax.psum_scatter(attn_part, 'tp', scatter_dimension=0, tiled=True)
        resid_rows = (x_rows.astype(jnp.float32) + attn_rows.astype(jnp.float32)).astype(jnp.bfloat16)
        normed_mlp = lax.all_gather(rms_norm(resid_rows, g_mlp), 'tp', axis=0, tiled=True)
        gate_proj = jnp.dot(normed_mlp, w_gate, preferred_element_type=jnp.float32)
        up_proj = jnp.dot(normed_mlp, w_up, preferred_element_type=jnp.float32)
        hidden = (jax.nn.silu(gate_proj) * up_proj).astype(jnp.bfloat16)
        down_part = jnp.dot(hidden, w_down, preferred_element_type=jnp.float32).astype(jnp.bfloat16)
        down_rows = lax.psum_scatter(down_part, 'tp', scatter_dimension=0, tiled=True)
        z_rows = (resid_rows.astype(jnp.float32) + down_rows.astype(jnp.float32)).astype(jnp.bfloat16)
        return z_rows[None]

    return jax.shard_map(local_layer, mesh=mesh,
                         in_specs=(row_spec, P(), head_cols, head_cols, head_cols, P('tp', None, None),
                                   P(), P(None, 'tp'), P(None, 'tp'), P('tp', None)),
                         out_specs=row_spec, check_vma=False)
```

profile of v0, /device:TPU:0, one launch (start us, length us, event | category | flops | bytes accessed | tf_op | source)
XLA Modules:
  0.0 1135.7 jit_solution(11022815784002712598)
XLA Ops:
  22.4 77.4 %all-gather.7.cloned.1.call-done = bf16[2048,3072]{1,0:T(8,128)(2,1)} async-done(((bf16[512,3072]{1,0:T(8,128)(2,1)}), bf16[2048,3072]{1,0:T(8,128)(2,1)}) %all-gather.7.cloned.1.call-update) | async-done | bytes 12582928 | tf_op jit(solution)/shard_map/all_gather | solution.py:68
  125.8 14.3 %fusion.128 = f32[2048,768]{0,1:S(1)} fusion(bf16[2048,3072]{1,0:T(8,128)(2,1)} %all-gather.7.cloned.1.call-done, bf16[3072,768]{0,1:T(8,128)(2,1)} %bitcast.160), kind=kOutput, calls=%fused_computation.133 | convolution fusion | flops 9663676416 | bytes 23592960
  146.1 44.4 %all-gather.11.cloned.1.call-done = bf16[8192,2,128]{0,2,1:T(8,128)(2,1)} async-done(((bf16[2048,2,128]{0,2,1:T(8,128)(2,1)}), bf16[8192,2,128]{0,2,1:T(8,128)(2,1)}) %all-gather.11.cloned.1.call-update) | async-done | bytes 4194320 | tf_op jit(solution)/shard_map/all_gather | solution.py:75
  206.7 64.6 %all-gather.13.cloned.1.call-done = bf16[8192,2,128]{2,0,1:T(8,128)(2,1)} async-done(((bf16[2048,2,128]{2,0,1:T(8,128)(2,1)}), bf16[8192,2,128]{2,0,1:T(8,128)(2,1)}) %all-gather.13.cloned.1.call-update) | async-done | bytes 4194320 | tf_op jit(solution)/shard_map/all_gather | solution.py:76
  274.7 149.6 %while.21 = (s32[]{:T(128)}, bf16[4,256,2,3,128]{4,1,0,3,2:T(8,128)(2,1)S(1)}, s32[4]{0:T(128)S(1)}, s32[1024]{0:T(1024)S(1)}, s32[4,1024]{1,0:T(4,128)S(1)}, /*...) while((s32[]{:T(128)}, ...), condition=%wide.region_4.5_spmd, body=%wide.region_1.4_spmd.sunk | while | flops 3291870208 | bytes 93148376 | solution.py:53
  277.1 12.3 %fusion.155 = (f32[2,256,3]{1,2,0:T(4,128)S(1)}, f32[2,256,3,4096]{3,1,2,0:T(8,128)}) fusion(pred[256,4096]{1,0:T(8,128)(4,1)S(1)} %broadcast_compare_fusion.5, bf16[4096,2,128]{2,0,1:T(8,128)(2,1)} %get-tuple-element.335, bf16[1024,2,3,128]{0,3,2,1:T(8,128)(2,1)} %get-tuple-element.334, s32[]{:T(128)S(6)} %select_n.202), kind=kOutput, calls=%fused_computation.3.clone.1 | convolution fusion | flops 1629485568 | bytes 28710916 | tf_op jit(solution)/shard_map/while/body/eval_jaxpr/qgrd,kgd->gqrk/dot_general | solution.py:45
  289.5 11.9 %fusion.156 = f32[2,256,3]{1,2,0:T(4,128)S(1)} fusion(f32[2,256,3,4096]{3,1,2,0:T(8,128)} %get-tuple-element.261, f32[2,256,3]{1,2,0:T(4,128)S(1)} %get-tuple-element.262, pred[256,4096]{1,0:T(8,128)(4,1)S(1)} %broadcast_compare_fusion.5), kind=kLoop, calls=%fused_computation.4.clone.1 | loop fusion | flops 25164288 | bytes 26226688 | tf_op jit(solution)/shard_map/while/body/eval_jaxpr/reduce_sum | solution.py:49
  314.4 12.3 %fusion.155 = (f32[2,256,3]{1,2,0:T(4,128)S(1)}, f32[2,256,3,4096]{3,1,2,0:T(8,128)}) fusion(pred[256,4096]{1,0:T(8,128)(4,1)S(1)} %broadcast_compare_fusion.5, bf16[4096,2,128]{2,0,1:T(8,128)(2,1)} %get-tuple-element.335, bf16[1024,2,3,128]{0,3,2,1:T(8,128)(2,1)} %get-tuple-element.334, s32[]{:T(128)S(6)} %select_n.202), kind=kOutput, calls=%fused_computation.3.clone.1 | convolution fusion | flops 1629485568 | bytes 28710916 | tf_op jit(solution)/shard_map/while/body/eval_jaxpr/qgrd,kgd->gqrk/dot_general | solution.py:45
  326.8 11.9 %fusion.156 = f32[2,256,3]{1,2,0:T(4,128)S(1)} fusion(f32[2,256,3,4096]{3,1,2,0:T(8,128)} %get-tuple-element.261, f32[2,256,3]{1,2,0:T(4,128)S(1)} %get-tuple-element.262, pred[256,4096]{1,0:T(8,128)(4,1)S(1)} %broadcast_compare_fusion.5), kind=kLoop, calls=%fused_computation.4.clone.1 | loop fusion | flops 25164288 | bytes 26226688 | tf_op jit(solution)/shard_map/while/body/eval_jaxpr/reduce_sum | solution.py:49
  351.7 12.3 %fusion.155 = (f32[2,256,3]{1,2,0:T(4,128)S(1)}, f32[2,256,3,4096]{3,1,2,0:T(8,128)}) fusion(pred[256,4096]{1,0:T(8,128)(4,1)S(1)} %broadcast_compare_fusion.5, bf16[4096,2,128]{2,0,1:T(8,128)(2,1)} %get-tuple-element.335, bf16[1024,2,3,128]{0,3,2,1:T(8,128)(2,1)} %get-tuple-element.334, s32[]{:T(128)S(6)} %select_n.202), kind=kOutput, calls=%fused_computation.3.clone.1 | convolution fusion | flops 1629485568 | bytes 28710916 | tf_op jit(solution)/shard_map/while/body/eval_jaxpr/qgrd,kgd->gqrk/dot_general | solution.py:45
  364.0 11.9 %fusion.156 = f32[2,256,3]{1,2,0:T(4,128)S(1)} fusion(f32[2,256,3,4096]{3,1,2,0:T(8,128)} %get-tuple-element.261, f32[2,256,3]{1,2,0:T(4,128)S(1)} %get-tuple-element.262, pred[256,4096]{1,0:T(8,128)(4,1)S(1)} %broadcast_compare_fusion.5), kind=kLoop, calls=%fused_computation.4.clone.1 | loop fusion | flops 25164288 | bytes 26226688 | tf_op jit(solution)/shard_map/while/body/eval_jaxpr/reduce_sum | solution.py:49
  389.0 12.3 %fusion.155 = (f32[2,256,3]{1,2,0:T(4,128)S(1)}, f32[2,256,3,4096]{3,1,2,0:T(8,128)}) fusion(pred[256,4096]{1,0:T(8,128)(4,1)S(1)} %broadcast_compare_fusion.5, bf16[4096,2,128]{2,0,1:T(8,128)(2,1)} %get-tuple-element.335, bf16[1024,2,3,128]{0,3,2,1:T(8,128)(2,1)} %get-tuple-element.334, s32[]{:T(128)S(6)} %select_n.202), kind=kOutput, calls=%fused_computation.3.clone.1 | convolution fusion | flops 1629485568 | bytes 28710916 | tf_op jit(solution)/shard_map/while/body/eval_jaxpr/qgrd,kgd->gqrk/dot_general | solution.py:45
  431.6 282.0 %while.22 = (s32[]{:T(128)}, bf16[4,256,2,3,128]{4,1,0,3,2:T(8,128)(2,1)S(1)}, s32[4]{0:T(128)S(1)}, s32[1024]{0:T(1024)}, bf16[1024,2,3,128]{0,3,2,1:T(8,128)(2...) while((s32[]{:T(128)}, ...), condition=%wide.region_8.9_spmd.clone, body=%wide.region_5.8_spmd.clone.sunk | while | flops 6583514112 | bytes 177050832 | solution.py:53
  435.0 22.5 %fusion.161 = (f32[2,256,3]{1,2,0:T(4,128)S(1)}, f32[2,256,3,8192]{3,1,2,0:T(8,128)}) fusion(pred[256,8192]{1,0:T(8,128)(4,1)S(1)} %broadcast_compare_fusion.6, bf16[8192,2,128]{2,0,1:T(8,128)(2,1)} %get-tuple-element.299, bf16[1024,2,3,128]{0,3,2,1:T(8,128)(2,1)} %get-tuple-element.298, s32[]{:T(128)S(6)} %select_n.209), kind=kOutput, calls=%fused_computation.24.clone.1 | convolution fusion | flops 3258972672 | bytes 57022468 | tf_op jit(solution)/shard_map/while/body/eval_jaxpr/qgrd,kgd->gqrk/dot_general | solution.py:45
  457.5 22.9 %fusion.162 = f32[2,256,3]{1,2,0:T(4,128)S(1)} fusion(f32[2,256,3,8192]{3,1,2,0:T(8,128)} %get-tuple-element.270, f32[2,256,3]{1,2,0:T(4,128)S(1)} %get-tuple-element.271, pred[256,8192]{1,0:T(8,128)(4,1)} %copy-done.2), kind=kLoop, calls=%fused_computation.25.clone.1 | loop fusion | flops 50330112 | bytes 52441088 | tf_op jit(solution)/shard_map/while/body/eval_jaxpr/reduce_sum | solution.py:49
  480.4 21.8 %fusion.163 = bf16[4,256,2,3,128]{4,1,0,3,2:T(8,128)(2,1)S(1)} fusion(bf16[4,256,2,3,128]{4,1,0,3,2:T(8,128)(2,1)S(1)} %get-tuple-element.284, s32[]{:T(128)} %get-tuple-element.283, bf16[8192,2,128]{2,0,1:T(8,128)(2,1)} %get-tuple-element.300, f32[2,256,3,8192]{3,1,2,0:T(8,128)} %get-tuple-element.270, f32[2,256,3]{1,2,0:T(4,128)S(1)} %get-tuple-element.271, ...), kind=kOutput, calls=%fused_computation.37.clone.1 | convolution fusion | flops 3271950336 | bytes 57032708 | tf_op jit(solution)/shard_map/while/body/eval_jaxpr/gqrk,kgd->gqrd/dot_general | solution.py:50
  505.5 22.5 %fusion.161 = (f32[2,256,3]{1,2,0:T(4,128)S(1)}, f32[2,256,3,8192]{3,1,2,0:T(8,128)}) fusion(pred[256,8192]{1,0:T(8,128)(4,1)S(1)} %broadcast_compare_fusion.6, bf16[8192,2,128]{2,0,1:T(8,128)(2,1)} %get-tuple-element.299, bf16[1024,2,3,128]{0,3,2,1:T(8,128)(2,1)} %get-tuple-element.298, s32[]{:T(128)S(6)} %select_n.209), kind=kOutput, calls=%fused_computation.24.clone.1 | convolution fusion | flops 3258972672 | bytes 57022468 | tf_op jit(solution)/shard_map/while/body/eval_jaxpr/qgrd,kgd->gqrk/dot_general | solution.py:45
  528.0 22.9 %fusion.162 = f32[2,256,3]{1,2,0:T(4,128)S(1)} fusion(f32[2,256,3,8192]{3,1,2,0:T(8,128)} %get-tuple-element.270, f32[2,256,3]{1,2,0:T(4,128)S(1)} %get-tuple-element.271, pred[256,8192]{1,0:T(8,128)(4,1)} %copy-done.2), kind=kLoop, calls=%fused_computation.25.clone.1 | loop fusion | flops 50330112 | bytes 52441088 | tf_op jit(solution)/shard_map/while/body/eval_jaxpr/reduce_sum | solution.py:49
  550.9 21.8 %fusion.163 = bf16[4,256,2,3,128]{4,1,0,3,2:T(8,128)(2,1)S(1)} fusion(bf16[4,256,2,3,128]{4,1,0,3,2:T(8,128)(2,1)S(1)} %get-tuple-element.284, s32[]{:T(128)} %get-tuple-element.283, bf16[8192,2,128]{2,0,1:T(8,128)(2,1)} %get-tuple-element.300, f32[2,256,3,8192]{3,1,2,0:T(8,128)} %get-tuple-element.270, f32[2,256,3]{1,2,0:T(4,128)S(1)} %get-tuple-element.271, ...), kind=kOutput, calls=%fused_computation.37.clone.1 | convolution fusion | flops 3271950336 | bytes 57032708 | tf_op jit(solution)/shard_map/while/body/eval_jaxpr/gqrk,kgd->gqrd/dot_general | solution.py:50
  575.9 22.5 %fusion.161 = (f32[2,256,3]{1,2,0:T(4,128)S(1)}, f32[2,256,3,8192]{3,1,2,0:T(8,128)}) fusion(pred[256,8192]{1,0:T(8,128)(4,1)S(1)} %broadcast_compare_fusion.6, bf16[8192,2,128]{2,0,1:T(8,128)(2,1)} %get-tuple-element.299, bf16[1024,2,3,128]{0,3,2,1:T(8,128)(2,1)} %get-tuple-element.298, s32[]{:T(128)S(6)} %select_n.209), kind=kOutput, calls=%fused_computation.24.clone.1 | convolution fusion | flops 3258972672 | bytes 57022468 | tf_op jit(solution)/shard_map/while/body/eval_jaxpr/qgrd,kgd->gqrk/dot_general | solution.py:45
  598.4 22.9 %fusion.162 = f32[2,256,3]{1,2,0:T(4,128)S(1)} fusion(f32[2,256,3,8192]{3,1,2,0:T(8,128)} %get-tuple-element.270, f32[2,256,3]{1,2,0:T(4,128)S(1)} %get-tuple-element.271, pred[256,8192]{1,0:T(8,128)(4,1)} %copy-done.2), kind=kLoop, calls=%fused_computation.25.clone.1 | loop fusion | flops 50330112 | bytes 52441088 | tf_op jit(solution)/shard_map/while/body/eval_jaxpr/reduce_sum | solution.py:49
  621.3 21.8 %fusion.163 = bf16[4,256,2,3,128]{4,1,0,3,2:T(8,128)(2,1)S(1)} fusion(bf16[4,256,2,3,128]{4,1,0,3,2:T(8,128)(2,1)S(1)} %get-tuple-element.284, s32[]{:T(128)} %get-tuple-element.283, bf16[8192,2,128]{2,0,1:T(8,128)(2,1)} %get-tuple-element.300, f32[2,256,3,8192]{3,1,2,0:T(8,128)} %get-tuple-element.270, f32[2,256,3]{1,2,0:T(4,128)S(1)} %get-tuple-element.271, ...), kind=kOutput, calls=%fused_computation.37.clone.1 | convolution fusion | flops 3271950336 | bytes 57032708 | tf_op jit(solution)/shard_map/while/body/eval_jaxpr/gqrk,kgd->gqrd/dot_general | solution.py:50
  646.4 22.5 %fusion.161 = (f32[2,256,3]{1,2,0:T(4,128)S(1)}, f32[2,256,3,8192]{3,1,2,0:T(8,128)}) fusion(pred[256,8192]{1,0:T(8,128)(4,1)S(1)} %broadcast_compare_fusion.6, bf16[8192,2,128]{2,0,1:T(8,128)(2,1)} %get-tuple-element.299, bf16[1024,2,3,128]{0,3,2,1:T(8,128)(2,1)} %get-tuple-element.298, s32[]{:T(128)S(6)} %select_n.209), kind=kOutput, calls=%fused_computation.24.clone.1 | convolution fusion | flops 3258972672 | bytes 57022468 | tf_op jit(solution)/shard_map/while/body/eval_jaxpr/qgrd,kgd->gqrk/dot_general | solution.py:45
  668.9 22.9 %fusion.162 = f32[2,256,3]{1,2,0:T(4,128)S(1)} fusion(f32[2,256,3,8192]{3,1,2,0:T(8,128)} %get-tuple-element.270, f32[2,256,3]{1,2,0:T(4,128)S(1)} %get-tuple-element.271, pred[256,8192]{1,0:T(8,128)(4,1)} %copy-done.2), kind=kLoop, calls=%fused_computation.25.clone.1 | loop fusion | flops 50330112 | bytes 52441088 | tf_op jit(solution)/shard_map/while/body/eval_jaxpr/reduce_sum | solution.py:49
  691.8 21.8 %fusion.163 = bf16[4,256,2,3,128]{4,1,0,3,2:T(8,128)(2,1)S(1)} fusion(bf16[4,256,2,3,128]{4,1,0,3,2:T(8,128)(2,1)S(1)} %get-tuple-element.284, s32[]{:T(128)} %get-tuple-element.283, bf16[8192,2,128]{2,0,1:T(8,128)(2,1)} %get-tuple-element.300, f32[2,256,3,8192]{3,1,2,0:T(8,128)} %get-tuple-element.270, f32[2,256,3]{1,2,0:T(4,128)S(1)} %get-tuple-element.271, ...), kind=kOutput, calls=%fused_computation.37.clone.1 | convolution fusion | flops 3271950336 | bytes 57032708 | tf_op jit(solution)/shard_map/while/body/eval_jaxpr/gqrk,kgd->gqrd/dot_general | solution.py:50
  713.6 14.4 %bitcast_convert_fusion = bf16[2048,3072]{1,0:T(8,128)(2,1)} fusion(bf16[6,128,3072]{2,1,0:T(8,128)(2,1)} %param.19, bf16[1024,6,128]{2,0,1:T(8,128)(2,1)S(1)} %bitcast.165, bf16[1024,6,128]{2,0,1:T(8,128)(2,1)} %bitcast.166), kind=kOutput, calls=%fused_computation.61 | convolution fusion | flops 9676259328 | bytes 20447232 | tf_op jit(solution)/shard_map/shk,hkd->sd/dot_general | solution.py:88
  728.7 97.6 %reduce-scatter.3.cloned.1.call-done = bf16[512,3072]{1,0:T(8,128)(2,1)} async-done(((bf16[2048,3072]{1,0:T(8,128)(2,1)}), bf16[512,3072]{1,0:T(8,128)(2,1)}) %reduce-scatter.3.cloned.1.call-update) | async-done | bytes 3145744 | tf_op jit(solution)/shard_map/reduce_scatter | solution.py:89
  835.6 82.2 %all-gather.9.cloned.1.call-done = bf16[2048,3072]{1,0:T(8,128)(2,1)} async-done(((bf16[512,3072]{1,0:T(8,128)(2,1)}), bf16[2048,3072]{1,0:T(8,128)(2,1)}) %all-gather.9.cloned.1.call-update) | async-done | bytes 12582928 | tf_op jit(solution)/shard_map/all_gather | solution.py:91
  917.8 34.7 %fusion.130 = f32[2048,2048]{1,0:T(8,128)} fusion(bf16[2048,3072]{1,0:T(8,128)(2,1)} %all-gather.9.cloned.1.call-done, bf16[3072,2048]{1,0:T(8,128)(2,1)} %param.21), kind=kOutput, calls=%fused_computation.135 | convolution fusion | flops 25769803776 | bytes 41943040 | tf_op jit(solution)/shard_map/dot_general | solution.py:92
  952.5 38.1 %multiply_convert_fusion = bf16[2048,2048]{1,0:T(8,128)(2,1)} fusion(f32[2048,2048]{1,0:T(8,128)} %fusion.130, bf16[2048,3072]{1,0:T(8,128)(2,1)} %all-gather.9.cloned.1.call-done, bf16[3072,2048]{1,0:T(8,128)(2,1)} %param.22), kind=kOutput, calls=%fused_computation.62 | convolution fusion | flops 25794969600 | bytes 50331648 | tf_op jit(solution)/shard_map/dot_general | solution.py:93
  990.6 30.8 %convolution_convert_fusion = bf16[2048,3072]{1,0:T(8,128)(2,1)} fusion(bf16[2048,2048]{1,0:T(8,128)(2,1)} %multiply_convert_fusion, bf16[2048,3072]{1,0:T(8,128)(2,1)S(1)} %bitcast.174), kind=kOutput, calls=%fused_computation.65 | convolution fusion | flops 25776095232 | bytes 33554432 | tf_op jit(solution)/shard_map/dot_general | solution.py:95
  1021.4 99.7 %reduce-scatter.5.cloned.1.call-done = bf16[512,3072]{1,0:T(8,128)(2,1)} async-done(((bf16[2048,3072]{1,0:T(8,128)(2,1)}), bf16[512,3072]{1,0:T(8,128)(2,1)}) %reduce-scatter.5.cloned.1.call-update) | async-done | bytes 3145744 | tf_op jit(solution)/shard_map/reduce_scatter | solution.py:96
  (126 shorter events, 163.6 us)
Async XLA Ops:
  6.5 109.8 %copy-start = (bf16[3072,2,128]{2,1,0:T(2,128)(2,1)S(1)}, bf16[3072,2,128]{2,1,0:T(2,128)(2,1)}, u32[]{:S(2)}) copy-start(bf16[3072,2,128]{2,1,0:T(2,128)(2,1)} %param.18) | copy-start | bytes 4718596
  6.5 93.3 %all-gather.7.cloned.1.call-start = ((), (), s32[]{:S(2)}) async-start(), calls=%async_computation.2 | async-start | bytes 15728640 | tf_op jit(solution)/shard_map/all_gather | solution.py:68
  7.4 7.5 copy-start.7
  14.8 175.6 %all-gather.11.cloned.1.call-start = ((), (), s32[]{:S(2)}) async-start(), calls=%async_computation.6 | async-start | bytes 5242880 | tf_op jit(solution)/shard_map/all_gather | solution.py:75
  106.7 1.2 copy-start.4
  109.6 161.7 %all-gather.13.cloned.1.call-start = ((), (), s32[]{:S(2)}) async-start(), calls=%async_computation.7 | async-start | bytes 5242880 | tf_op jit(solution)/shard_map/all_gather | solution.py:76
  124.8 701.5 %reduce-scatter.3.cloned.1.call-start = ((), (), s32[]{:S(2)}) async-start(), calls=%async_computation.3 | async-start | bytes 15728640 | tf_op jit(solution)/shard_map/reduce_scatter | solution.py:89
  140.9 1.2 copy-start.5
  289.5 11.9 %copy-start.6 = (bf16[4096,2,128]{2,0,1:T(8,128)(2,1)S(1)}, bf16[4096,2,128]{2,0,1:T(8,128)(2,1)}, u32[]{:S(2)}) copy-start(bf16[4096,2,128]{2,0,1:T(8,128)(2,1)} %get-tuple-element.336) | copy-start | bytes 6291460 | tf_op jit(solution)/shard_map/while
  326.8 11.9 %copy-start.6 = (bf16[4096,2,128]{2,0,1:T(8,128)(2,1)S(1)}, bf16[4096,2,128]{2,0,1:T(8,128)(2,1)}, u32[]{:S(2)}) copy-start(bf16[4096,2,128]{2,0,1:T(8,128)(2,1)} %get-tuple-element.336) | copy-start | bytes 6291460 | tf_op jit(solution)/shard_map/while
  364.0 11.9 %copy-start.6 = (bf16[4096,2,128]{2,0,1:T(8,128)(2,1)S(1)}, bf16[4096,2,128]{2,0,1:T(8,128)(2,1)}, u32[]{:S(2)}) copy-start(bf16[4096,2,128]{2,0,1:T(8,128)(2,1)} %get-tuple-element.336) | copy-start | bytes 6291460 | tf_op jit(solution)/shard_map/while
  401.3 11.9 %copy-start.6 = (bf16[4096,2,128]{2,0,1:T(8,128)(2,1)S(1)}, bf16[4096,2,128]{2,0,1:T(8,128)(2,1)}, u32[]{:S(2)}) copy-start(bf16[4096,2,128]{2,0,1:T(8,128)(2,1)} %get-tuple-element.336) | copy-start | bytes 6291460 | tf_op jit(solution)/shard_map/while
  424.3 6.9 copy-start.8
  435.0 22.5 %copy-start.2 = (pred[256,8192]{1,0:T(8,128)(4,1)}, pred[256,8192]{1,0:T(8,128)(4,1)S(1)}, u32[]{:S(2)}) copy-start(pred[256,8192]{1,0:T(8,128)(4,1)S(1)} %broadcast_compare_fusion.6) | copy-start | bytes 6291460 | tf_op jit(solution)/shard_map/while
  505.5 22.5 %copy-start.2 = (pred[256,8192]{1,0:T(8,128)(4,1)}, pred[256,8192]{1,0:T(8,128)(4,1)S(1)}, u32[]{:S(2)}) copy-start(pred[256,8192]{1,0:T(8,128)(4,1)S(1)} %broadcast_compare_fusion.6) | copy-start | bytes 6291460 | tf_op jit(solution)/shard_map/while
  575.9 22.5 %copy-start.2 = (pred[256,8192]{1,0:T(8,128)(4,1)}, pred[256,8192]{1,0:T(8,128)(4,1)S(1)}, u32[]{:S(2)}) copy-start(pred[256,8192]{1,0:T(8,128)(4,1)S(1)} %broadcast_compare_fusion.6) | copy-start | bytes 6291460 | tf_op jit(solution)/shard_map/while
  646.4 22.5 %copy-start.2 = (pred[256,8192]{1,0:T(8,128)(4,1)}, pred[256,8192]{1,0:T(8,128)(4,1)S(1)}, u32[]{:S(2)}) copy-start(pred[256,8192]{1,0:T(8,128)(4,1)S(1)} %broadcast_compare_fusion.6) | copy-start | bytes 6291460 | tf_op jit(solution)/shard_map/while
  728.0 0.7 copy-start.9
  728.0 189.8 %all-gather.9.cloned.1.call-start = ((), (), s32[]{:S(2)}) async-start(), calls=%async_computation.4 | async-start | bytes 15728640 | tf_op jit(solution)/shard_map/all_gather | solution.py:91
  826.2 4.1 copy-start.3
  835.5 285.6 %reduce-scatter.5.cloned.1.call-start = ((), (), s32[]{:S(2)}) async-start(), calls=%async_computation.5 | async-start | bytes 15728640 | tf_op jit(solution)/shard_map/reduce_scatter | solution.py:96
  917.8 72.8 %slice-start = ((s8[12582912]{0:T(1024)(128)(4,1)}), s8[4194304]{0:T(1024)(128)(4,1)S(1)}, s32[]{:S(2)}) async-start(s8[12582912]{0:T(1024)(128)(4,1)} %bitcast.173), calls=%async_computation.8 | async-start | bytes 8388608
  917.8 72.8 %slice-start.1 = ((s8[12582912]{0:T(1024)(128)(4,1)}), s8[4194304]{0:T(1024)(128)(4,1)S(1)}, s32[]{:S(2)}) async-start(s8[12582912]{0:T(1024)(128)(4,1)} %bitcast.173), calls=%async_computation.9 | async-start | bytes 8388608
  952.5 38.1 %slice-start.2 = ((s8[12582912]{0:T(1024)(128)(4,1)}), s8[4194304]{0:T(1024)(128)(4,1)S(1)}, s32[]{:S(2)}) async-start(s8[12582912]{0:T(1024)(128)(4,1)} %bitcast.173), calls=%async_computation.10 | async-start | bytes 8388608
  1021.4 107.0 %copy-start.1 = (bf16[3072,2,128]{2,1,0:T(2,128)(2,1)S(1)}, bf16[3072,2,128]{2,1,0:T(2,128)(2,1)}, u32[]{:S(2)}) copy-start(bf16[3072,2,128]{2,1,0:T(2,128)(2,1)} %param.18) | copy-start | bytes 4718596
Sparse Core Ops, SparseCore 0:
  14.9 84.8 all-gather.6
  109.7 80.7 all-gather.10
  192.0 79.2 all-gather.12
  728.1 98.0 reduce-scatter.2
  835.7 82.0 all-gather.8
  1021.5 99.5 reduce-scatter.4
where the time goes:
time: 1140 us
  waiting for transfers between devices  466 us (41%)
  matrix products  418 us (37%)
  other arithmetic  182 us (16%)
  local copies, waits for them, and re-layouts  49.2 us (4%)
  between operations  14.1 us (1%)
    dot_general x8, matrix products, one_tile(): jnp.einsum('qgrd,kgd->gqrk', q_tile, keys, preferred_element_type=jnp.flo...  139 us
    reduce_sum x8, other arithmetic, one_tile(): row_sum = jnp.sum(weights, axis=-1, keepdims=True)  139 us
    dot_general x8, matrix products, one_tile(): jnp.einsum('gqrk,kgd->gqrd', weights.astype(jnp.bfloat16), values, prefer...  131 us
    reduce_scatter x1, waiting for transfers between devices, local_layer(): lax.psum_scatter(down_part, 'tp', scatter_dimension=0, tiled=True)  99.7 us
    reduce_scatter x1, waiting for transfers between devices, local_layer(): lax.psum_scatter(attn_part, 'tp', scatter_dimension=0, tiled=True)  97.6 us
    all_gather x1, waiting for transfers between devices, local_layer(): lax.all_gather(rms_norm(resid_rows, g_mlp), 'tp', axis=0, tiled=True)  82.2 us
    all_gather x1, waiting for transfers between devices, local_layer(): normed = lax.all_gather(rms_norm(x_rows, g_attn), 'tp', axis=0, tiled=True)  77.4 us
    all_gather x1, waiting for transfers between devices, local_layer(): v_seq = lax.all_gather(v_all, 'cp', axis=0, tiled=False)  64.6 us
  transfers between devices with their start and end apart: 6, of which 6 were waited for; matrix products, arithmetic and copies ran while one was open for 5% of the time, Pallas kernels for 0%

commit v1 on v0

v1 whole, which is shorter than its diff:
```python
import functools
import jax
import jax.numpy as jnp
from jax import lax
from jax.experimental import pallas as pl
from jax.experimental.pallas import tpu as pltpu
from jax.sharding import PartitionSpec as P

NORM_EPS = 1e-5
ROPE_THETA = 500000.0
N_CHUNKS = 4
KEY_BLOCK = 1024
LOG2_E = 1.4426950408889634
REL = (0, 2, 1, 3)


def rms_norm(rows_f32, gain_vec):
    mean_sq = jnp.mean(rows_f32 * rows_f32, axis=-1, keepdims=True)
    return (rows_f32 * lax.rsqrt(mean_sq + NORM_EPS) * gain_vec.astype(jnp.float32)).astype(jnp.bfloat16)


def proj_kernel(a_ref, w0_ref, w1_ref, cos_ref, sin_ref, o_ref, *, rope_heads):
    w = jnp.concatenate([w0_ref[...], w1_ref[...]], axis=1)
    acc = jnp.dot(a_ref[...], w, preferred_element_type=jnp.float32).astype(jnp.bfloat16)
    for h in range(2):
        head = acc[:, h * 128:(h + 1) * 128]
        if h < rope_heads:
            head = head.astype(jnp.float32)
            head = (head * cos_ref[...] + pltpu.roll(head, 64, 1) * sin_ref[...]).astype(jnp.bfloat16)
        o_ref[:, h * 128:(h + 1) * 128] = head


def project(a, w0, w1, first, second, cos, sin, rope_heads, steps):
    rows, depth = a.shape
    cols = steps * 256
    return pl.pallas_call(
        functools.partial(proj_kernel, rope_heads=rope_heads),
        grid=(steps,),
        in_specs=[pl.BlockSpec((rows, depth), lambda n: (0, 0)),
                  pl.BlockSpec((depth, 128), lambda n: (0, first(n))),
                  pl.BlockSpec((depth, 128), lambda n: (0, second(n))),
                  pl.BlockSpec((rows, 128), lambda n: (0, 0)),
                  pl.BlockSpec((rows, 128), lambda n: (0, 0))],
        out_specs=pl.BlockSpec((rows, 256), lambda n: (0, n)),
        out_shape=jax.ShapeDtypeStruct((rows, cols), jnp.bfloat16),
        compiler_params=pltpu.CompilerParams(vmem_limit_bytes=32 * 2**20),
        cost_estimate=pl.CostEstimate(flops=2 * rows * depth * cols, transcendentals=0,
                                      bytes_accessed=2 * (rows * depth + depth * cols + rows * cols)),
    )(a, w0, w1, cos, sin)


def norm_kernel(x_ref, mine_ref, got_ref, gain_ref, resid_ref, b_ref):
    added = (mine_ref[...] + got_ref[...].astype(jnp.float32)).astype(jnp.bfloat16)
    resid = (x_ref[...].astype(jnp.float32) + added.astype(jnp.float32)).astype(jnp.bfloat16)
    resid_ref[...] = resid
    rows = resid.astype(jnp.float32)
    mean_sq = jnp.mean(rows * rows, axis=1, keepdims=True)
    b_ref[...] = (rows * lax.rsqrt(mean_sq + NORM_EPS) * gain_ref[...].astype(jnp.float32)).astype(jnp.bfloat16)


def add_norm(x_rows, mine, got, gain, chunk):
    rows, width = got.shape
    whole = pl.BlockSpec((rows, width), lambda i: (0, 0))
    shape = jax.ShapeDtypeStruct((rows, width), jnp.bfloat16)
    return pl.pallas_call(
        norm_kernel,
        grid=(1,),
        in_specs=[pl.BlockSpec((rows, width), lambda i: (chunk, 0)), whole, whole,
                  pl.BlockSpec((1, width), lambda i: (0, 0))],
        out_specs=[whole, whole],
        out_shape=[shape, shape],
        compiler_params=pltpu.CompilerParams(vmem_limit_bytes=16 * 2**20),
        cost_estimate=pl.CostEstimate(flops=8 * rows * width, transcendentals=rows, bytes_accessed=12 * rows * width),
    )(x_rows, mine, got, gain.reshape(1, width))


def pair_add_kernel(part_ref, got_ref, mine_ref, send_ref):
    rows = mine_ref.shape[0]
    total = part_ref[...].astype(jnp.float32) + got_ref[...].astype(jnp.float32)
    mine_ref[...] = total[:rows]
    send_ref[...] = total[rows:].astype(jnp.bfloat16)


def pair_add(part, got):
    rows, width = part.shape
    block = width // 2
    whole = pl.BlockSpec((rows, block), lambda i: (0, i))
    half = pl.BlockSpec((rows // 2, block), lambda i: (0, i))
    return pl.pallas_call(
        pair_add_kernel,
        grid=(2,),
        in_specs=[whole, whole],
        out_specs=[half, half],
        out_shape=[jax.ShapeDtypeStruct((rows // 2, width), jnp.float32),
                   jax.ShapeDtypeStruct((rows // 2, width), jnp.bfloat16)],
        compiler_params=pltpu.CompilerParams(vmem_limit_bytes=24 * 2**20),
        cost_estimate=pl.CostEstimate(flops=2 * rows * width, transcendentals=0, bytes_accessed=7 * rows * width),
    )(part, got)


def gate_up_kernel(*refs):
    *bs, gate_ref, up_ref, u_ref, b_scr = refs
    rows = bs[0].shape[0]

    @pl.when(pl.program_id(0) == 0)
    def _():
        for i, b in enumerate(bs):
            b_scr[i * rows:(i + 1) * rows, :] = b[...]

    gate = jnp.dot(b_scr[...], gate_ref[...], preferred_element_type=jnp.float32)
    up = jnp.dot(b_scr[...], up_ref[...], preferred_element_type=jnp.float32)
    u_ref[...] = (gate * jax.nn.sigmoid(gate) * up).astype(jnp.bfloat16)


def gate_up(bs, w_gate, w_up):
    rows, width = bs[0].shape
    tall = len(bs) * rows
    hidden = w_gate.shape[1]
    block = 256
    piece = pl.BlockSpec((rows, width), lambda n: (0, 0))
    cols = pl.BlockSpec((width, block), lambda n: (0, n))
    return pl.pallas_call(
        gate_up_kernel,
        grid=(hidden // block,),
        in_specs=[piece] * len(bs) + [cols] * 2,
        out_specs=pl.BlockSpec((tall, block), lambda n: (0, n)),
        out_shape=jax.ShapeDtypeStruct((tall, hidden), jnp.bfloat16),
        scratch_shapes=[pltpu.VMEM((tall, width), jnp.bfloat16)],
        compiler_params=pltpu.CompilerParams(vmem_limit_bytes=63 * 2**20),
        cost_estimate=pl.CostEstimate(flops=4 * tall * width * hidden, transcendentals=tall * hidden,
                                      bytes_accessed=4 * width * hidden + 2 * tall * (width + hidden)),
    )(*bs, w_gate, w_up)


def down_kernel(u_ref, w_ref, *out_refs):
    half = out_refs[0].shape[0]
    out = jnp.dot(u_ref[...], w_ref[...], preferred_element_type=jnp.float32).astype(jnp.bfloat16)
    for i, ref in enumerate(out_refs):
        ref[...] = out[i * half:(i + 1) * half]


def down(u, w_down, first, count, half):
    hidden = u.shape[1]
    width = w_down.shape[1]
    rows = count * half
    block = 512
    out = pl.BlockSpec((half, block), lambda n: (0, n))
    shape = jax.ShapeDtypeStruct((half, width), jnp.bfloat16)
    return pl.pallas_call(
        down_kernel,
        grid=(width // block,),
        in_specs=[pl.BlockSpec((rows, hidden), lambda n: (first, 0)), pl.BlockSpec((hidden, block), lambda n: (0, n))],
        out_specs=[out] * count,
        out_shape=[shape] * count,
        compiler_params=pltpu.CompilerParams(vmem_limit_bytes=63 * 2**20),
        cost_estimate=pl.CostEstimate(flops=2 * rows * width * hidden, transcendentals=0,
                                      bytes_accessed=2 * (width * hidden + rows * (width + hidden))),
    )(u, w_down)


def flash_kernel(info_ref, q0, q1, q2, q3, *rest, rows, chunk, cp_size, dim):
    n_src = 4 * (2 * cp_size - 1)
    sources = rest[:n_src]
    o_p, o_q, kv_scr, q_scr, m_scr, l_scr, acc_scr, sems = rest[n_src:]
    g = pl.program_id(0)
    me, cp = info_ref[0], info_ref[1]
    n_keys = KEY_BLOCK
    heads = 3
    last = 2 * cp_size - 1 - cp

    def each_copy(h, act):
        for i, src in enumerate(sources):
            u, slot = divmod(i, 2 * cp_size - 1)
            j = cp + slot - (cp_size - 1)
            t = me ^ REL[u]
            piece = jnp.where(t < 2, j, 2 * cp_size - 1 - j)

            @pl.when((j >= 0) & (j < cp_size) & (piece <= last))
            def _():
                start = pl.multiple_of(piece * 1024 + (t & 1) * 512, 512)
                act(pltpu.make_async_copy(src.at[:, pl.ds(h * 2 * dim, 2 * dim)], kv_scr.at[h, pl.ds(start, 512)],
                                          sems.at[h, i]))

    @pl.when(g == 0)
    def _():
        each_copy(0, lambda c: c.start())
        each_copy(1, lambda c: c.start())
        each_copy(0, lambda c: c.wait())

    @pl.when(g == 1)
    def _():
        each_copy(1, lambda c: c.wait())

    scale = (dim ** -0.5) * LOG2_E

    def step(first, starts):
        k = kv_scr[g, pl.ds(first, n_keys), 0:dim]
        v = kv_scr[g, pl.ds(first, n_keys), dim:2 * dim]
        s = lax.dot_general(q_scr[...], k, (((1,), (1,)), ((), ())), preferred_element_type=jnp.float32) * scale
        if starts is not None:
            k_pos = first + lax.broadcasted_iota(jnp.int32, (rows, n_keys), 1)
            parts = []
            for i in range(2):
                visible = starts[i] + lax.broadcasted_iota(jnp.int32, (rows, n_keys), 0) >= k_pos
                parts += [jnp.where(visible, s[n * rows:(n + 1) * rows], -1e30) for n in range(i * heads, (i + 1) * heads)]
            s = jnp.concatenate(parts, axis=0)
        m_old = m_scr[...]
        m_new = jnp.maximum(m_old, jnp.max(s, axis=1, keepdims=True))
        m_scr[...] = m_new
        alpha = jnp.exp2(m_old - m_new)
        p = jnp.exp2(s - jnp.tile(m_new, (1, n_keys // 128)))
        part = p[:, 0:128]
        for n in range(1, n_keys // 128):
            part = part + p[:, n * 128:(n + 1) * 128]
        l_scr[...] = l_scr[...] * alpha + part
        acc_scr[...] = acc_scr[...] * alpha + jnp.dot(p.astype(jnp.bfloat16), v, preferred_element_type=jnp.float32)

    for far, q_pair in enumerate(((q0, q2), (q1, q3))):
        t = me ^ (2 * far)
        piece = jnp.where(t < 2, cp, last)
        starts = [piece * 1024 + ((me ^ i) & 1) * 512 + chunk * rows for i in range(2)]
        for i in range(2):
            for h in range(heads):
                n = i * heads + h
                q_scr[n * rows:(n + 1) * rows, :] = q_pair[i][:, h * dim:(h + 1) * dim]
        m_scr[...] = jnp.full_like(m_scr, -1e30)
        l_scr[...] = jnp.zeros_like(l_scr)
        acc_scr[...] = jnp.zeros_like(acc_scr)
        n_full = piece * (1024 // n_keys)

        @pl.loop(0, n_full)
        def _(b):
            step(pl.multiple_of(b * n_keys, n_keys), None)

        @pl.loop(n_full, n_full + 1024 // n_keys)
        def _(b):
            step(pl.multiple_of(b * n_keys, n_keys), starts)

        out = (acc_scr[...] / jnp.sum(l_scr[...], axis=1, keepdims=True)).astype(jnp.bfloat16)
        for i, o_ref in enumerate((o_p, o_q)):
            for h in range(heads):
                n = i * heads + h
                o_ref[far * rows:(far + 1) * rows, h * dim:(h + 1) * dim] = out[n * rows:(n + 1) * rows]


def flash(info, qs, sources, chunk, cp_size):
    rows = qs[0].shape[0] // N_CHUNKS
    dim = 128
    width = 3 * dim
    seq = cp_size * 2048
    q_spec = pl.BlockSpec((rows, width), lambda g: (chunk, g))
    o_spec = pl.BlockSpec((2 * rows, width), lambda g: (0, g))
    o_shape = jax.ShapeDtypeStruct((2 * rows, 2 * width), jnp.bfloat16)
    pairs = 4 * rows * seq // 2
    stat = pltpu.VMEM((6 * rows, 128), jnp.float32)
    return pl.pallas_call(
        functools.partial(flash_kernel, rows=rows, chunk=chunk, cp_size=cp_size, dim=dim),
        grid=(2,),
        in_specs=[pl.BlockSpec(memory_space=pltpu.SMEM)] + [q_spec] * 4 + [pl.BlockSpec(memory_space=pl.ANY)] * len(sources),
        out_specs=[o_spec, o_spec],
        out_shape=[o_shape, o_shape],
        scratch_shapes=[pltpu.VMEM((2, seq, 2 * dim), jnp.bfloat16),
                        pltpu.VMEM((6 * rows, dim), jnp.bfloat16),
                        stat, stat, stat,
                        pltpu.SemaphoreType.DMA((2, len(sources)))],
        compiler_params=pltpu.CompilerParams(vmem_limit_bytes=60 * 2**20),
        cost_estimate=pl.CostEstimate(flops=8 * pairs * 6 * dim, transcendentals=pairs * 6,
                                      bytes_accessed=seq * 4 * dim * 2),
    )(info, *qs, *sources)


def solution(mesh):
    cp_size = mesh.shape['cp']
    row_spec = P('dp', ('cp', 'tp'), None)
    head_cols = P(None, 'tp', None)
    f32, bf16 = jnp.float32, jnp.bfloat16

    def core_swap(v):
        return lax.ppermute(v, 'tp', [(t, t ^ 1) for t in range(4)])

    def y_swap(v):
        return lax.ppermute(v, 'tp', [(t, t ^ 2) for t in range(4)])

    def z_gather(own):
        right, left = own, own
        slots = {0: own}
        for hop in range(1, cp_size):
            right = lax.ppermute(right, 'cp', [(i, i + 1) for i in range(hop - 1, cp_size - 1)])
            left = lax.ppermute(left, 'cp', [(i, i - 1) for i in range(1, cp_size - hop + 1)])
            slots[-hop], slots[hop] = right, left
        return [slots[d] for d in range(1 - cp_size, cp_size)]

    def local_layer(x, g_attn, w_q, w_k, w_v, w_o, g_mlp, w_gate, w_up, w_down):
        x_rows = x[0]
        n_rows, width = x_rows.shape
        me = lax.axis_index('tp')
        cp = lax.axis_index('cp')
        info = jnp.stack([me, cp]).astype(jnp.int32)
        w_q = w_q.reshape(width, -1)
        w_k = w_k.reshape(width, -1)
        w_v = w_v.reshape(width, -1)
        w_o = w_o.reshape(-1, width)

        inv_freq = ROPE_THETA ** (-2.0 * jnp.arange(64, dtype=f32) / 128)
        tables = []
        for rel in REL:
            t = me ^ rel
            start = jnp.where(t < 2, cp, 2 * cp_size - 1 - cp) * 1024 + (t & 1) * 512
            angles = (start + jnp.arange(n_rows, dtype=jnp.int32)).astype(f32)[:, None] * inv_freq[None, :]
            cos, sin = jnp.cos(angles), jnp.sin(angles)
            tables.append((jnp.concatenate([cos, cos], axis=1), jnp.concatenate([-sin, sin], axis=1)))

        a_self = rms_norm(x_rows.astype(f32), g_attn)
        a_y = y_swap(a_self)
        a_core = core_swap(a_self)

        def kv_of(a, i):
            return project(a, w_k, w_v, lambda n: n, lambda n: n, *tables[i], 1, 2)

        def q_of(a, i):
            return project(a, w_q, w_q, lambda n: 2 * n, lambda n: 2 * n + 1, *tables[i], 2, 3)

        kv_self = z_gather(kv_of(a_self, 0))
        kv_core = z_gather(kv_of(a_core, 2))
        q_self = q_of(a_self, 0)
        q_core = q_of(a_core, 2)
        a_diag = core_swap(a_y)
        kv_y = z_gather(kv_of(a_y, 1))
        kv_diag = z_gather(kv_of(a_diag, 3))
        q_y = q_of(a_y, 1)
        q_diag = q_of(a_diag, 3)

        rows = n_rows // N_CHUNKS
        qs = (q_self, q_y, q_core, q_diag)
        sources = tuple(kv_self + kv_y + kv_core + kv_diag)

        def dot(a, b):
            return jnp.dot(a, b, preferred_element_type=f32)

        def after(values, *first):
            return lax.optimization_barrier((values, first))[0]

        def residual(base, mine, got):
            return (base.astype(f32) + (mine + got.astype(f32)).astype(bf16).astype(f32)).astype(bf16)

        resid, b_self, b_y, b_diag = {}, {}, {}, {}
        mine1, got1, mine2, got2 = {}, {}, {}, {}

        def attention(c, *first):
            o_p, o_q = flash(info, after(qs, *first), sources, c, cp_size)
            part_q = dot(o_q, w_o).astype(bf16)
            got = core_swap(part_q)
            mine1[c], send = pair_add(dot(after(o_p, part_q), w_o), got)
            got1[c] = y_swap(send)
            return send

        def spread(c):
            resid[c], b_self[c] = add_norm(x_rows, mine1[c], got1[c], g_mlp, c)
            b_y[c] = y_swap(b_self[c])
            b_diag[c] = core_swap(b_y[c])

        def gate_of(chunks, *first):
            bs = []
            for c in chunks:
                bs += [b_self[c], b_y[c], core_swap(b_self[c]), b_diag[c]]
            return gate_up(after(tuple(bs), *first), w_gate, w_up)

        def return_rows(c, part_p, part_q):
            got = core_swap(part_q)
            mine2[c], send = pair_add(part_p, got)
            got2[c] = y_swap(send)

        sent = attention(0)
        sent = attention(1, sent)
        spread(0)
        sent = attention(2, sent, b_self[0])
        spread(1)
        sent = attention(3, sent, b_self[1])
        spread(2)
        hidden = gate_of((0, 1), sent, b_self[2])
        spread(3)
        parts = down(hidden, w_down, 0, 4, 2 * rows)
        return_rows(0, *parts[:2])
        return_rows(1, *parts[2:])
        hidden = gate_of((2, 3))
        for i in range(2):
            parts = down(hidden, w_down, i, 2, 2 * rows)
            return_rows(2 + i, *parts)
        outs = [residual(resid[c], mine2[c], got2[c]) for c in range(N_CHUNKS)]
        return jnp.concatenate(outs, axis=0)[None]

    return jax.shard_map(local_layer, mesh=mesh,
                         in_specs=(row_spec, P(), head_cols, head_cols, head_cols, P('tp', None, None),
                                   P(), P(None, 'tp'), P(None, 'tp'), P('tp', None)),
                         out_specs=row_spec, check_vma=False)
```

time: 1140 us -> 718 us (0.63)
  matrix products: 418 us -> 31.3 us
  Pallas kernels: 0 us -> 276 us
  waiting for transfers between devices: 466 us -> 271 us
  other arithmetic: 182 us -> 14.5 us
  starting transfers between devices: 0.42 us -> 76 us
  between operations: 14.1 us -> 1.51 us
  local copies, waits for them, and re-layouts: 49.2 us -> 37.5 us
    dot_general x21 -> x8, matrix products: 397 us -> 31.3 us  [dot(): return jnp.dot(a, b, preferred_element_type=f32)]
    pallas_call x0 -> x29, Pallas kernels: none -> 276 us  [the longest x4 115 us: flash(): pl.pallas_call(functools.partial(flash_kernel, rows=rows, chunk=chunk, cp...]
    ppermute x0 -> x55, waiting for transfers between devices: none -> 271 us  [the longest x13 220 us: y_swap(): return lax.ppermute(v, 'tp', [(t, t ^ 2) for t in range(4)])]
    all_gather x4 -> x0, waiting for transfers between devices: 269 us -> none  [the longest x1 82.2 us: local_layer(): lax.all_gather(rms_norm(resid_rows, g_mlp), 'tp', axis=0, tiled=True)]
    reduce_scatter x2 -> x0, waiting for transfers between devices: 197 us -> none  [the longest x1 99.7 us: local_layer(): lax.psum_scatter(down_part, 'tp', scatter_dimension=0, tiled=True)]
    reduce_sum x8 -> x0, other arithmetic: 139 us -> none  [one_tile(): row_sum = jnp.sum(weights, axis=-1, keepdims=True)]
    ppermute x0 -> x55, starting transfers between devices: none -> 76 us  [the longest x12 40.7 us: z_gather(): lax.ppermute(right, 'cp', [(i, i + 1) for i in range(hop - 1, cp_size - 1)])]
    unnamed x2 -> x0, matrix products: 21.2 us -> none
  transfers between devices with their start and end apart: 6 -> 55, of which waited for: 6 -> 18; matrix products, arithmetic and copies ran while one was open for 5% -> 5% of each run, Pallas kernels for 0% -> 22%
where the time goes in v1:
time: 718 us; the launch traced here: 708 us
  Pallas kernels  276 us (38%)
  waiting for transfers between devices  271 us (38%)
  starting transfers between devices  76 us (11%)
  local copies, waits for them, and re-layouts  37.5 us (5%)
  matrix products  31.3 us (4%)
  other arithmetic  14.5 us (2%)
    ppermute x13, waiting for transfers between devices, y_swap(): return lax.ppermute(v, 'tp', [(t, t ^ 2) for t in range(4)])  220 us
    pallas_call x4, Pallas kernels, flash(): pl.pallas_call(functools.partial(flash_kernel, rows=rows, chunk=chunk, cp...  115 us
    pallas_call x2, Pallas kernels, gate_up(): pl.pallas_call(gate_up_kernel, grid=(hidden // block,), in_specs=[piece]...  65.3 us
    pallas_call x3, Pallas kernels, down(): pl.pallas_call(down_kernel, grid=(width // block,), in_specs=[pl.BlockSpe...  41.4 us
    ppermute x12, starting transfers between devices, z_gather(): lax.ppermute(right, 'cp', [(i, i + 1) for i in range(hop - 1, cp_size - 1)])  40.7 us
    pallas_call x8, Pallas kernels, project(): pl.pallas_call(functools.partial(proj_kernel, rope_heads=rope_heads), gri...  40.5 us
    ppermute x12, waiting for transfers between devices, z_gather(): lax.ppermute(left, 'cp', [(i, i - 1) for i in range(1, cp_size - hop + 1)])  40.2 us
    dot_general x8, matrix products, dot(): return jnp.dot(a, b, preferred_element_type=f32)  31.3 us
  transfers between devices with their start and end apart: 55, of which 18 were waited for; matrix products, arithmetic and copies ran while one was open for 5% of the time, Pallas kernels for 22%

profile of v1, /device:TPU:0, one launch (start us, length us, event | category | flops | bytes accessed | tf_op | source)
XLA Modules:
  0.0 707.8 jit_solution(14536232570631065594)
XLA Ops:
  9.4 68.4 %collective-permute-done.a_ref = bf16[512,3072]{1,0:T(8,128)(2,1)} collective-permute-done((bf16[512,3072]{1,0:T(8,128)(2,1)}, bf16[512,3072]{1,0:T(8,128)(2,1)}, u32[]{:S(2)}, u32[]{:S(2)}) %collective-permute-start) | collective-permute-done | bytes 3145760 | tf_op jit(solution)/shard_map/ppermute | solution.py:282
  92.1 10.5 %collective-permute-done.3.rest_2_ = bf16[512,512]{1,0:T(8,128)(2,1)S(1)} collective-permute-done((bf16[512,512]{1,0:T(8,128)(2,1)S(1)}, bf16[512,512]{1,0:T(8,128)(2,1)S(1)}, u32[]{:S(2)}, u32[]{:S(2)}) %collective-permute-start.3) | collective-permute-done | bytes 524320 | tf_op jit(solution)/shard_map/ppermute | solution.py:288
  109.1 12.7 %collective-permute-done.7.rest_5_ = bf16[512,512]{1,0:T(8,128)(2,1)S(1)} collective-permute-done((bf16[512,512]{1,0:T(8,128)(2,1)S(1)}, bf16[512,512]{1,0:T(8,128)(2,1)S(1)}, u32[]{:S(2)}, u32[]{:S(2)}) %collective-permute-start.7) | collective-permute-done | bytes 524320 | tf_op jit(solution)/shard_map/ppermute | solution.py:289
  137.9 16.7 %collective-permute-start.15 = (bf16[512,512]{1,0:T(8,128)(2,1)S(1)}, bf16[512,512]{1,0:T(8,128)(2,1)}, u32[]{:S(2)}, u32[]{:S(2)}) collective-permute-start(bf16[512,512]{1,0:T(8,128)(2,1)S(1)} %shard_map.106.rest_17_), channel_id=1, source_target_pairs={{0,4},{4,8},{8,12},{1,5},{5,9},{9,13},{2,6},{6,10},{10,14},{3,7},{... | collective-permute-start | bytes 1572872 | tf_op jit(solution)/shard_map/ppermute | solution.py:288
  163.3 7.0 collective-permute-start.21
  178.8 8.4 %collective-permute-done.13.rest_12_ = bf16[512,512]{1,0:T(8,128)(2,1)S(1)} collective-permute-done((bf16[512,512]{1,0:T(8,128)(2,1)S(1)}, bf16[512,512]{1,0:T(8,128)(2,1)S(1)}, u32[]{:S(2)}, u32[]{:S(2)}) %collective-permute-start.13) | collective-permute-done | bytes 524320 | tf_op jit(solution)/shard_map/ppermute | solution.py:289
  190.1 8.3 %collective-permute-done.24.rest_25_ = bf16[512,512]{1,0:T(8,128)(2,1)} collective-permute-done((bf16[512,512]{1,0:T(8,128)(2,1)S(1)}, bf16[512,512]{1,0:T(8,128)(2,1)}, u32[]{:S(2)}, u32[]{:S(2)}) %collective-permute-start.24) | collective-permute-done | bytes 524320 | tf_op jit(solution)/shard_map/ppermute | solution.py:289
  199.8 6.7 copy.12
  206.5 6.6 copy.13.w0_ref.w1_ref
  218.0 5.9 shard_map.100.q0
  230.3 5.8 shard_map.101.q1
  237.0 5.8 shard_map.102.q2
  243.6 5.7 shard_map.103.q3
  256.4 28.7 %shard_map.108 = (bf16[256,768]{1,0:T(8,128)(2,1)}, bf16[256,768]{1,0:T(8,128)(2,1)}) custom-call(s32[2]{0:T(128)} %pad_add_fusion.info_ref, bf16[512,768]{1,0:T(8,128)(2,1)} %copy-done.35, bf16[512,768]{1,0:T(8,128)(2,1)} %copy-done.36, bf16[512,768]{1,0:T(8,128)(2,1)} %copy-done.37, bf16[512,768]{1,0:T(8,128)(2,1)} %copy-done.38, ...), custom_call_target="tpu_custom_call" | custom-call | flops 12884901888 | bytes 8388608 | tf_op jit(solution)/shard_map/pallas_call | solution.py:256
  296.0 28.7 %shard_map.111 = (bf16[256,768]{1,0:T(8,128)(2,1)}, bf16[256,768]{1,0:T(8,128)(2,1)}) custom-call(s32[2]{0:T(128)} %pad_add_fusion.info_ref, bf16[512,768]{1,0:T(8,128)(2,1)} %copy-done.35, bf16[512,768]{1,0:T(8,128)(2,1)} %copy-done.36, bf16[512,768]{1,0:T(8,128)(2,1)} %copy-done.37, bf16[512,768]{1,0:T(8,128)(2,1)} %copy-done.38, ...), custom_call_target="tpu_custom_call" | custom-call | flops 12884901888 | bytes 8388608 | tf_op jit(solution)/shard_map/pallas_call | solution.py:256
  334.6 14.1 %collective-permute-done.28.got_ref = bf16[128,3072]{1,0:T(8,128)(2,1)S(1)} collective-permute-done((bf16[128,3072]{1,0:T(8,128)(2,1)S(1)}, bf16[128,3072]{1,0:T(8,128)(2,1)S(1)}, u32[]{:S(2)}, u32[]{:S(2)}) %collective-permute-start.28) | collective-permute-done | bytes 786464 | tf_op jit(solution)/shard_map/ppermute | solution.py:282
  354.0 29.1 %shard_map.114 = (bf16[256,768]{1,0:T(8,128)(2,1)}, bf16[256,768]{1,0:T(8,128)(2,1)}) custom-call(s32[2]{0:T(128)} %pad_add_fusion.info_ref, bf16[512,768]{1,0:T(8,128)(2,1)} %copy-done.35, bf16[512,768]{1,0:T(8,128)(2,1)} %copy-done.36, bf16[512,768]{1,0:T(8,128)(2,1)} %copy-done.37, bf16[512,768]{1,0:T(8,128)(2,1)} %copy-done.38, ...), custom_call_target="tpu_custom_call" | custom-call | flops 12884901888 | bytes 8388608 | tf_op jit(solution)/shard_map/pallas_call | solution.py:256
  392.6 14.5 %collective-permute-done.33.got_ref = bf16[128,3072]{1,0:T(8,128)(2,1)S(1)} collective-permute-done((bf16[128,3072]{1,0:T(8,128)(2,1)S(1)}, bf16[128,3072]{1,0:T(8,128)(2,1)S(1)}, u32[]{:S(2)}, u32[]{:S(2)}) %collective-permute-start.33) | collective-permute-done | bytes 786464 | tf_op jit(solution)/shard_map/ppermute | solution.py:282
  412.3 28.9 %shard_map.116 = (bf16[256,768]{1,0:T(8,128)(2,1)}, bf16[256,768]{1,0:T(8,128)(2,1)}) custom-call(s32[2]{0:T(128)} %pad_add_fusion.info_ref, bf16[512,768]{1,0:T(8,128)(2,1)} %copy-done.35, bf16[512,768]{1,0:T(8,128)(2,1)} %copy-done.36, bf16[512,768]{1,0:T(8,128)(2,1)} %copy-done.37, bf16[512,768]{1,0:T(8,128)(2,1)} %copy-done.38, ...), custom_call_target="tpu_custom_call" | custom-call | flops 12884901888 | bytes 8388608 | tf_op jit(solution)/shard_map/pallas_call | solution.py:256
  448.9 16.9 %collective-permute-done.29.refs_1_ = bf16[128,3072]{1,0:T(8,128)(2,1)S(1)} collective-permute-done((bf16[128,3072]{1,0:T(8,128)(2,1)S(1)}, bf16[128,3072]{1,0:T(8,128)(2,1)S(1)}, u32[]{:S(2)}, u32[]{:S(2)}) %collective-permute-start.29) | collective-permute-done | bytes 786464 | tf_op jit(solution)/shard_map/ppermute | solution.py:282
  469.9 12.8 %collective-permute-done.34.refs_5_ = bf16[128,3072]{1,0:T(8,128)(2,1)S(1)} collective-permute-done((bf16[128,3072]{1,0:T(8,128)(2,1)S(1)}, bf16[128,3072]{1,0:T(8,128)(2,1)S(1)}, u32[]{:S(2)}, u32[]{:S(2)}) %collective-permute-start.34) | collective-permute-done | bytes 786464 | tf_op jit(solution)/shard_map/ppermute | solution.py:282
  483.9 15.0 %collective-permute-done.39.got_ref = bf16[128,3072]{1,0:T(8,128)(2,1)S(1)} collective-permute-done((bf16[128,3072]{1,0:T(8,128)(2,1)S(1)}, bf16[128,3072]{1,0:T(8,128)(2,1)S(1)}, u32[]{:S(2)}, u32[]{:S(2)}) %collective-permute-start.39) | collective-permute-done | bytes 786464 | tf_op jit(solution)/shard_map/ppermute | solution.py:282
  502.6 16.8 %collective-permute-done.47.got_ref = bf16[128,3072]{1,0:T(8,128)(2,1)S(1)} collective-permute-done((bf16[128,3072]{1,0:T(8,128)(2,1)S(1)}, bf16[128,3072]{1,0:T(8,128)(2,1)S(1)}, u32[]{:S(2)}, u32[]{:S(2)}) %collective-permute-start.47) | collective-permute-done | bytes 786464 | tf_op jit(solution)/shard_map/ppermute | solution.py:282
  523.4 32.8 %shard_map.119.u_ref = bf16[1024,2048]{1,0:T(8,128)(2,1)} custom-call(bf16[128,3072]{1,0:T(8,128)(2,1)} %copy-done.43, bf16[128,3072]{1,0:T(8,128)(2,1)} %copy-done.56, bf16[128,3072]{1,0:T(8,128)(2,1)} %copy-done.58, bf16[128,3072]{1,0:T(8,128)(2,1)} %copy-done.59, bf16[128,3072]{1,0:T(8,128)(2,1)} %copy-done.45, bf16[128,3072]{1,0:T(8,128)(2,1)} %copy-done.57, ...), custom_call_target="tpu_custom_call" | custom-call | flops 25769803776 | bytes 35651584 | tf_op jit(solution)/shard_map/pallas_call | solution.py:122
  556.8 18.0 %shard_map.120 = (bf16[256,3072]{1,0:T(8,128)(2,1)}, bf16[256,3072]{1,0:T(8,128)(2,1)}, bf16[256,3072]{1,0:T(8,128)(2,1)}, bf16[256,3072]{1,0:T(8,128)(2,1)}) custom-call(bf16[1024,2048]{1,0:T(8,128)(2,1)} %shard_map.119.u_ref, bf16[2048,3072]{1,0:T(8,128)(2,1)} %w_ref.5), custom_call_target="tpu_custom_call" | custom-call | flops 12884901888 | bytes 23068672 | tf_op jit(solution)/shard_map/pallas_call | solution.py:149
  575.4 32.6 %shard_map.124.u_ref = bf16[1024,2048]{1,0:T(8,128)(2,1)} custom-call(bf16[128,3072]{1,0:T(8,128)(2,1)} %get-tuple-element.140.refs_0_, bf16[128,3072]{1,0:T(8,128)(2,1)} %collective-permute-done.44.refs_1_, bf16[128,3072]{1,0:T(8,128)(2,1)} %collective-permute-done.45.refs_2_, bf16[128,3072]{1,0:T(8,128)(2,1)} %collective-permute-done.46.refs_3_, ...), custom_call_target="tpu_custom_call" | custom-call | flops 25769803776 | bytes 35651584 | tf_op jit(solution)/shard_map/pallas_call | solution.py:122
  607.9 11.7 %shard_map.127 = (bf16[256,3072]{1,0:T(8,128)(2,1)}, bf16[256,3072]{1,0:T(8,128)(2,1)}) custom-call(bf16[1024,2048]{1,0:T(8,128)(2,1)} %shard_map.124.u_ref, bf16[2048,3072]{1,0:T(8,128)(2,1)} %w_ref.5), custom_call_target="tpu_custom_call" | custom-call | flops 6442450944 | bytes 17825792 | tf_op jit(solution)/shard_map/pallas_call | solution.py:149
  619.8 11.7 %shard_map.125 = (bf16[256,3072]{1,0:T(8,128)(2,1)}, bf16[256,3072]{1,0:T(8,128)(2,1)}) custom-call(bf16[1024,2048]{1,0:T(8,128)(2,1)} %shard_map.124.u_ref, bf16[2048,3072]{1,0:T(8,128)(2,1)} %w_ref.5), custom_call_target="tpu_custom_call" | custom-call | flops 6442450944 | bytes 17825792 | tf_op jit(solution)/shard_map/pallas_call | solution.py:149
  641.6 14.1 %collective-permute-done.43 = bf16[128,3072]{1,0:T(8,128)(2,1)S(1)} collective-permute-done((bf16[128,3072]{1,0:T(8,128)(2,1)S(1)}, bf16[128,3072]{1,0:T(8,128)(2,1)S(1)}, u32[]{:S(2)}, u32[]{:S(2)}) %collective-permute-start.43) | collective-permute-done | bytes 786464 | tf_op jit(solution)/shard_map/ppermute | solution.py:282
  657.4 15.2 %collective-permute-done.41 = bf16[128,3072]{1,0:T(8,128)(2,1)S(1)} collective-permute-done((bf16[128,3072]{1,0:T(8,128)(2,1)S(1)}, bf16[128,3072]{1,0:T(8,128)(2,1)S(1)}, u32[]{:S(2)}, u32[]{:S(2)}) %collective-permute-start.41) | collective-permute-done | bytes 786464 | tf_op jit(solution)/shard_map/ppermute | solution.py:282
  672.8 16.6 %collective-permute-done.54 = bf16[128,3072]{1,0:T(8,128)(2,1)S(1)} collective-permute-done((bf16[128,3072]{1,0:T(8,128)(2,1)S(1)}, bf16[128,3072]{1,0:T(8,128)(2,1)S(1)}, u32[]{:S(2)}, u32[]{:S(2)}) %collective-permute-start.54) | collective-permute-done | bytes 786464 | tf_op jit(solution)/shard_map/ppermute | solution.py:282
  689.7 15.8 %collective-permute-done.52 = bf16[128,3072]{1,0:T(8,128)(2,1)S(1)} collective-permute-done((bf16[128,3072]{1,0:T(8,128)(2,1)S(1)}, bf16[128,3072]{1,0:T(8,128)(2,1)S(1)}, u32[]{:S(2)}, u32[]{:S(2)}) %collective-permute-start.52) | collective-permute-done | bytes 786464 | tf_op jit(solution)/shard_map/ppermute | solution.py:282
  (301 shorter events, 164.1 us)
Async XLA Ops:
  6.4 71.4 %collective-permute-start = (bf16[512,3072]{1,0:T(8,128)(2,1)}, bf16[512,3072]{1,0:T(8,128)(2,1)}, u32[]{:S(2)}, u32[]{:S(2)}) collective-permute-start(bf16[512,3072]{1,0:T(8,128)(2,1)} %fusion.2.a_ref), channel_id=1, source_target_pairs={{0,2},{1,3},{2,0},{3,1},{4,6},{5,7},{6,4},{7,5},{8,10},{9,11},{10,... | collective-permute-start | bytes 9437192 | tf_op jit(solution)/shard_map/ppermute | solution.py:282
  9.4 122.8 %collective-permute-start.1 = (bf16[512,3072]{1,0:T(8,128)(2,1)}, bf16[512,3072]{1,0:T(8,128)(2,1)}, u32[]{:S(2)}, u32[]{:S(2)}) collective-permute-start(bf16[512,3072]{1,0:T(8,128)(2,1)} %fusion.2.a_ref), channel_id=1, source_target_pairs={{0,1},{1,0},{2,3},{3,2},{4,5},{5,4},{6,7},{7,6},{8,9},{9,8},{10,11... | collective-permute-start | bytes 9437192 | tf_op jit(solution)/shard_map/ppermute | solution.py:279
  77.8 60.1 %collective-permute-start.2 = (bf16[512,3072]{1,0:T(8,128)(2,1)}, bf16[512,3072]{1,0:T(8,128)(2,1)}, u32[]{:S(2)}, u32[]{:S(2)}) collective-permute-start(bf16[512,3072]{1,0:T(8,128)(2,1)} %collective-permute-done.a_ref), channel_id=1, source_target_pairs={{0,1},{1,0},{2,3},{3,2},{4,5},{5,4},{6,7},{7,6},{8,9},{9,8},{10,11... | collective-permute-start | bytes 9437192 | tf_op jit(solution)/shard_map/ppermute | solution.py:279
  108.4 50.7 %collective-permute-start.5 = (bf16[512,512]{1,0:T(8,128)(2,1)S(1)}, bf16[512,512]{1,0:T(8,128)(2,1)S(1)}, u32[]{:S(2)}, u32[]{:S(2)}) collective-permute-start(bf16[512,512]{1,0:T(8,128)(2,1)S(1)} %collective-permute-done.4.rest_1_), channel_id=1, source_target_pairs={{8,12},{9,13},{10,14},{11,15},{24,28},{25,29},{26,30},{27,31}} | collective-permute-start | bytes 1572872 | tf_op jit(solution)/shard_map/ppermute | solution.py:288
  121.9 41.4 %collective-permute-start.8 = (bf16[512,512]{1,0:T(8,128)(2,1)S(1)}, bf16[512,512]{1,0:T(8,128)(2,1)S(1)}, u32[]{:S(2)}, u32[]{:S(2)}) collective-permute-start(bf16[512,512]{1,0:T(8,128)(2,1)S(1)} %collective-permute-done.7.rest_5_), channel_id=1, source_target_pairs={{4,0},{5,1},{6,2},{7,3},{20,16},{21,17},{22,18},{23,19}} | collective-permute-start | bytes 1572872 | tf_op jit(solution)/shard_map/ppermute | solution.py:289
  127.6 32.9 %collective-permute-start.9 = (bf16[512,512]{1,0:T(8,128)(2,1)S(1)}, bf16[512,512]{1,0:T(8,128)(2,1)S(1)}, u32[]{:S(2)}, u32[]{:S(2)}) collective-permute-start(bf16[512,512]{1,0:T(8,128)(2,1)S(1)} %shard_map.105.rest_10_), channel_id=1, source_target_pairs={{0,4},{4,8},{8,12},{1,5},{5,9},{9,13},{2,6},{6,10},{10,14},{3,7},{... | collective-permute-start | bytes 1572872 | tf_op jit(solution)/shard_map/ppermute | solution.py:288
  132.2 29.8 %collective-permute-start.12 = (bf16[512,512]{1,0:T(8,128)(2,1)S(1)}, bf16[512,512]{1,0:T(8,128)(2,1)S(1)}, u32[]{:S(2)}, u32[]{:S(2)}) collective-permute-start(bf16[512,512]{1,0:T(8,128)(2,1)S(1)} %shard_map.105.rest_10_), channel_id=1, source_target_pairs={{4,0},{8,4},{12,8},{5,1},{9,5},{13,9},{6,2},{10,6},{14,10},{7,3},{... | collective-permute-start | bytes 1572872 | tf_op jit(solution)/shard_map/ppermute | solution.py:289
  137.9 32.4 %collective-permute-start.15 = (bf16[512,512]{1,0:T(8,128)(2,1)S(1)}, bf16[512,512]{1,0:T(8,128)(2,1)}, u32[]{:S(2)}, u32[]{:S(2)}) collective-permute-start(bf16[512,512]{1,0:T(8,128)(2,1)S(1)} %shard_map.106.rest_17_), channel_id=1, source_target_pairs={{0,4},{4,8},{8,12},{1,5},{5,9},{9,13},{2,6},{6,10},{10,14},{3,7},{... | collective-permute-start | bytes 1572872 | tf_op jit(solution)/shard_map/ppermute | solution.py:288
  162.0 25.1 %collective-permute-start.13 = (bf16[512,512]{1,0:T(8,128)(2,1)S(1)}, bf16[512,512]{1,0:T(8,128)(2,1)S(1)}, u32[]{:S(2)}, u32[]{:S(2)}) collective-permute-start(bf16[512,512]{1,0:T(8,128)(2,1)S(1)} %collective-permute-done.12.rest_11_), channel_id=1, source_target_pairs={{4,0},{8,4},{5,1},{9,5},{6,2},{10,6},{7,3},{11,7},{20,16},{24,20},... | collective-permute-start | bytes 1572872 | tf_op jit(solution)/shard_map/ppermute | solution.py:289
  163.3 25.3 %collective-permute-start.21 = (bf16[512,512]{1,0:T(8,128)(2,1)S(1)}, bf16[512,512]{1,0:T(8,128)(2,1)}, u32[]{:S(2)}, u32[]{:S(2)}) collective-permute-start(bf16[512,512]{1,0:T(8,128)(2,1)S(1)} %shard_map.107.rest_24_), channel_id=1, source_target_pairs={{0,4},{4,8},{8,12},{1,5},{5,9},{9,13},{2,6},{6,10},{10,14},{3,7},{... | collective-permute-start | bytes 1572872 | tf_op jit(solution)/shard_map/ppermute | solution.py:288
  170.3 28.1 %collective-permute-start.24 = (bf16[512,512]{1,0:T(8,128)(2,1)S(1)}, bf16[512,512]{1,0:T(8,128)(2,1)}, u32[]{:S(2)}, u32[]{:S(2)}) collective-permute-start(bf16[512,512]{1,0:T(8,128)(2,1)S(1)} %shard_map.107.rest_24_), channel_id=1, source_target_pairs={{4,0},{8,4},{12,8},{5,1},{9,5},{13,9},{6,2},{10,6},{14,10},{7,3},{... | collective-permute-start | bytes 1572872 | tf_op jit(solution)/shard_map/ppermute | solution.py:289
  176.0 48.8 %collective-permute-start.16 = (bf16[512,512]{1,0:T(8,128)(2,1)}, bf16[512,512]{1,0:T(8,128)(2,1)}, u32[]{:S(2)}, u32[]{:S(2)}) collective-permute-start(bf16[512,512]{1,0:T(8,128)(2,1)} %collective-permute-done.15.rest_16_), channel_id=1, source_target_pairs={{4,8},{8,12},{5,9},{9,13},{6,10},{10,14},{7,11},{11,15},{20,24},{2... | collective-permute-start | bytes 1572872 | tf_op jit(solution)/shard_map/ppermute | solution.py:288
  177.5 48.8 %collective-permute-start.19 = (bf16[512,512]{1,0:T(8,128)(2,1)}, bf16[512,512]{1,0:T(8,128)(2,1)}, u32[]{:S(2)}, u32[]{:S(2)}) collective-permute-start(bf16[512,512]{1,0:T(8,128)(2,1)} %collective-permute-done.18.rest_18_), channel_id=1, source_target_pairs={{4,0},{8,4},{5,1},{9,5},{6,2},{10,6},{7,3},{11,7},{20,16},{24,20},... | collective-permute-start | bytes 1572872 | tf_op jit(solution)/shard_map/ppermute | solution.py:289
  187.1 39.8 %collective-permute-start.11 = (bf16[512,512]{1,0:T(8,128)(2,1)}, bf16[512,512]{1,0:T(8,128)(2,1)}, u32[]{:S(2)}, u32[]{:S(2)}) collective-permute-start(bf16[512,512]{1,0:T(8,128)(2,1)} %collective-permute-done.10.rest_8_), channel_id=1, source_target_pairs={{8,12},{9,13},{10,14},{11,15},{24,28},{25,29},{26,30},{27,31}} | collective-permute-start | bytes 1572872 | tf_op jit(solution)/shard_map/ppermute | solution.py:288
  188.7 39.6 %collective-permute-start.22 = (bf16[512,512]{1,0:T(8,128)(2,1)}, bf16[512,512]{1,0:T(8,128)(2,1)}, u32[]{:S(2)}, u32[]{:S(2)}) collective-permute-start(bf16[512,512]{1,0:T(8,128)(2,1)} %collective-permute-done.21.rest_23_), channel_id=1, source_target_pairs={{4,8},{8,12},{5,9},{9,13},{6,10},{10,14},{7,11},{11,15},{20,24},{2... | collective-permute-start | bytes 1572872 | tf_op jit(solution)/shard_map/ppermute | solution.py:288
  198.5 30.5 %collective-permute-start.25 = (bf16[512,512]{1,0:T(8,128)(2,1)}, bf16[512,512]{1,0:T(8,128)(2,1)}, u32[]{:S(2)}, u32[]{:S(2)}) collective-permute-start(bf16[512,512]{1,0:T(8,128)(2,1)} %collective-permute-done.24.rest_25_), channel_id=1, source_target_pairs={{4,0},{8,4},{5,1},{9,5},{6,2},{10,6},{7,3},{11,7},{20,16},{24,20},... | collective-permute-start | bytes 1572872 | tf_op jit(solution)/shard_map/ppermute | solution.py:289
  224.8 25.4 %collective-permute-start.14 = (bf16[512,512]{1,0:T(8,128)(2,1)S(1)}, bf16[512,512]{1,0:T(8,128)(2,1)S(1)}, u32[]{:S(2)}, u32[]{:S(2)}) collective-permute-start(bf16[512,512]{1,0:T(8,128)(2,1)S(1)} %copy-done.72), channel_id=1, source_target_pairs={{4,0},{5,1},{6,2},{7,3},{20,16},{21,17},{22,18},{23,19}} | collective-permute-start | bytes 1572872 | tf_op jit(solution)/shard_map/ppermute | solution.py:289
  227.0 24.9 %collective-permute-start.20 = (bf16[512,512]{1,0:T(8,128)(2,1)}, bf16[512,512]{1,0:T(8,128)(2,1)S(1)}, u32[]{:S(2)}, u32[]{:S(2)}) collective-permute-start(bf16[512,512]{1,0:T(8,128)(2,1)} %collective-permute-done.19.rest_19_), channel_id=1, source_target_pairs={{4,0},{5,1},{6,2},{7,3},{20,16},{21,17},{22,18},{23,19}} | collective-permute-start | bytes 1572872 | tf_op jit(solution)/shard_map/ppermute | solution.py:289
  229.0 27.4 %collective-permute-start.26 = (bf16[512,512]{1,0:T(8,128)(2,1)}, bf16[512,512]{1,0:T(8,128)(2,1)}, u32[]{:S(2)}, u32[]{:S(2)}) collective-permute-start(bf16[512,512]{1,0:T(8,128)(2,1)} %collective-permute-done.25.rest_26_), channel_id=1, source_target_pairs={{4,0},{5,1},{6,2},{7,3},{20,16},{21,17},{22,18},{23,19}} | collective-permute-start | bytes 1572872 | tf_op jit(solution)/shard_map/ppermute | solution.py:289
  445.2 37.4 %collective-permute-start.38 = (bf16[256,3072]{1,0:T(8,128)(2,1)S(1)}, bf16[256,3072]{1,0:T(8,128)(2,1)S(1)}, u32[]{:S(2)}, u32[]{:S(2)}) collective-permute-start(bf16[256,3072]{1,0:T(8,128)(2,1)S(1)} %convolution_convert_fusion), channel_id=1, source_target_pairs={{0,1},{1,0},{2,3},{3,2},{4,5},{5,4},{6,7},{7,6},{8,9},{9,8},{10,11... | collective-permute-start | bytes 4718600 | tf_op jit(solution)/shard_map/ppermute | solution.py:279
  446.9 35.8 %collective-permute-start.34 = (bf16[128,3072]{1,0:T(8,128)(2,1)S(1)}, bf16[128,3072]{1,0:T(8,128)(2,1)S(1)}, u32[]{:S(2)}, u32[]{:S(2)}) collective-permute-start(bf16[128,3072]{1,0:T(8,128)(2,1)S(1)} %copy-done.46), channel_id=1, source_target_pairs={{0,2},{1,3},{2,0},{3,1},{4,6},{5,7},{6,4},{7,5},{8,10},{9,11},{10,... | collective-permute-start | bytes 2359304 | tf_op jit(solution)/shard_map/ppermute | solution.py:282
  447.4 51.5 %collective-permute-start.39 = (bf16[128,3072]{1,0:T(8,128)(2,1)S(1)}, bf16[128,3072]{1,0:T(8,128)(2,1)S(1)}, u32[]{:S(2)}, u32[]{:S(2)}) collective-permute-start(bf16[128,3072]{1,0:T(8,128)(2,1)S(1)} %copy-done.48), channel_id=1, source_target_pairs={{0,2},{1,3},{2,0},{3,1},{4,6},{5,7},{6,4},{7,5},{8,10},{9,11},{10,... | collective-permute-start | bytes 2359304 | tf_op jit(solution)/shard_map/ppermute | solution.py:282
  448.9 53.0 %collective-permute-start.30 = (bf16[128,3072]{1,0:T(8,128)(2,1)S(1)}, bf16[128,3072]{1,0:T(8,128)(2,1)S(1)}, u32[]{:S(2)}, u32[]{:S(2)}) collective-permute-start(bf16[128,3072]{1,0:T(8,128)(2,1)S(1)} %copy-done.44), channel_id=1, source_target_pairs={{0,1},{1,0},{2,3},{3,2},{4,5},{5,4},{6,7},{7,6},{8,9},{9,8},{10,11... | collective-permute-start | bytes 2359304 | tf_op jit(solution)/shard_map/ppermute | solution.py:279
  465.8 36.7 %collective-permute-start.31 = (bf16[128,3072]{1,0:T(8,128)(2,1)S(1)}, bf16[128,3072]{1,0:T(8,128)(2,1)S(1)}, u32[]{:S(2)}, u32[]{:S(2)}) collective-permute-start(bf16[128,3072]{1,0:T(8,128)(2,1)S(1)} %collective-permute-done.29.refs_1_), channel_id=1, source_target_pairs={{0,1},{1,0},{2,3},{3,2},{4,5},{5,4},{6,7},{7,6},{8,9},{9,8},{10,11... | collective-permute-start | bytes 2359304 | tf_op jit(solution)/shard_map/ppermute | solution.py:279
  501.9 54.2 %collective-permute-start.44 = (bf16[128,3072]{1,0:T(8,128)(2,1)}, bf16[128,3072]{1,0:T(8,128)(2,1)}, u32[]{:S(2)}, u32[]{:S(2)}) collective-permute-start(bf16[128,3072]{1,0:T(8,128)(2,1)} %get-tuple-element.140.refs_0_), channel_id=1, source_target_pairs={{0,2},{1,3},{2,0},{3,1},{4,6},{5,7},{6,4},{7,5},{8,10},{9,11},{10,... | collective-permute-start | bytes 2359304 | tf_op jit(solution)/shard_map/ppermute | solution.py:282
  502.5 72.5 %collective-permute-start.45 = (bf16[128,3072]{1,0:T(8,128)(2,1)}, bf16[128,3072]{1,0:T(8,128)(2,1)}, u32[]{:S(2)}, u32[]{:S(2)}) collective-permute-start(bf16[128,3072]{1,0:T(8,128)(2,1)} %get-tuple-element.140.refs_0_), channel_id=1, source_target_pairs={{0,1},{1,0},{2,3},{3,2},{4,5},{5,4},{6,7},{7,6},{8,9},{9,8},{10,11... | collective-permute-start | bytes 2359304 | tf_op jit(solution)/shard_map/ppermute | solution.py:279
  521.8 34.9 %collective-permute-start.48 = (bf16[128,3072]{1,0:T(8,128)(2,1)}, bf16[128,3072]{1,0:T(8,128)(2,1)S(1)}, u32[]{:S(2)}, u32[]{:S(2)}) collective-permute-start(bf16[128,3072]{1,0:T(8,128)(2,1)} %get-tuple-element.144.refs_4_), channel_id=1, source_target_pairs={{0,2},{1,3},{2,0},{3,1},{4,6},{5,7},{6,4},{7,5},{8,10},{9,11},{10,... | collective-permute-start | bytes 2359304 | tf_op jit(solution)/shard_map/ppermute | solution.py:282
  574.8 57.0 %collective-permute-start.42 = (bf16[256,3072]{1,0:T(8,128)(2,1)}, bf16[256,3072]{1,0:T(8,128)(2,1)}, u32[]{:S(2)}, u32[]{:S(2)}) collective-permute-start(bf16[256,3072]{1,0:T(8,128)(2,1)} %get-tuple-element.134), channel_id=1, source_target_pairs={{0,1},{1,0},{2,3},{3,2},{4,5},{5,4},{6,7},{7,6},{8,9},{9,8},{10,11... | collective-permute-start | bytes 4718600 | tf_op jit(solution)/shard_map/ppermute | solution.py:279
  575.1 60.7 %collective-permute-start.40 = (bf16[256,3072]{1,0:T(8,128)(2,1)}, bf16[256,3072]{1,0:T(8,128)(2,1)}, u32[]{:S(2)}, u32[]{:S(2)}) collective-permute-start(bf16[256,3072]{1,0:T(8,128)(2,1)} %get-tuple-element.129), channel_id=1, source_target_pairs={{0,1},{1,0},{2,3},{3,2},{4,5},{5,4},{6,7},{7,6},{8,9},{9,8},{10,11... | collective-permute-start | bytes 4718600 | tf_op jit(solution)/shard_map/ppermute | solution.py:279
  637.6 35.0 %collective-permute-start.41 = (bf16[128,3072]{1,0:T(8,128)(2,1)S(1)}, bf16[128,3072]{1,0:T(8,128)(2,1)S(1)}, u32[]{:S(2)}, u32[]{:S(2)}) collective-permute-start(bf16[128,3072]{1,0:T(8,128)(2,1)S(1)} %get-tuple-element.131), channel_id=1, source_target_pairs={{0,2},{1,3},{2,0},{3,1},{4,6},{5,7},{6,4},{7,5},{8,10},{9,11},{10,... | collective-permute-start | bytes 2359304 | tf_op jit(solution)/shard_map/ppermute | solution.py:282
  641.0 48.4 %collective-permute-start.54 = (bf16[128,3072]{1,0:T(8,128)(2,1)S(1)}, bf16[128,3072]{1,0:T(8,128)(2,1)S(1)}, u32[]{:S(2)}, u32[]{:S(2)}) collective-permute-start(bf16[128,3072]{1,0:T(8,128)(2,1)S(1)} %get-tuple-element.156), channel_id=1, source_target_pairs={{0,2},{1,3},{2,0},{3,1},{4,6},{5,7},{6,4},{7,5},{8,10},{9,11},{10,... | collective-permute-start | bytes 2359304 | tf_op jit(solution)/shard_map/ppermute | solution.py:282
  656.8 48.7 %collective-permute-start.52 = (bf16[128,3072]{1,0:T(8,128)(2,1)S(1)}, bf16[128,3072]{1,0:T(8,128)(2,1)S(1)}, u32[]{:S(2)}, u32[]{:S(2)}) collective-permute-start(bf16[128,3072]{1,0:T(8,128)(2,1)S(1)} %get-tuple-element.151), channel_id=1, source_target_pairs={{0,2},{1,3},{2,0},{3,1},{4,6},{5,7},{6,4},{7,5},{8,10},{9,11},{10,... | collective-permute-start | bytes 2359304 | tf_op jit(solution)/shard_map/ppermute | solution.py:282
  (104 other events, 1311.3 us)

commit v2 on v1

--- a/solution.py
+++ b/solution.py
@@ -158,10 +158,11 @@
     )(u, w_down)
 
 
-def flash_kernel(info_ref, q0, q1, q2, q3, *rest, rows, chunk, cp_size, dim):
+def flash_kernel(info_ref, q0, q1, q2, q3, w_ref, *rest, rows, chunk, cp_size, dim):
     n_src = 4 * (2 * cp_size - 1)
     sources = rest[:n_src]
-    o_p, o_q, kv_scr, q_scr, m_scr, l_scr, acc_scr, sems = rest[n_src:]
+    part_p, part_q, kv_scr, q_scr, m_scr, l_scr, acc_scr, o_scr, w_scr, sems, w_sem = rest[n_src:]
+    w_copy = pltpu.make_async_copy(w_ref, w_scr, w_sem)
     g = pl.program_id(0)
     me, cp = info_ref[0], info_ref[1]
     n_keys = KEY_BLOCK
@@ -185,6 +186,7 @@
     def _():
         each_copy(0, lambda c: c.start())
         each_copy(1, lambda c: c.start())
+        w_copy.start()
         each_copy(0, lambda c: c.wait())
 
     @pl.when(g == 1)
@@ -215,14 +217,19 @@
         l_scr[...] = l_scr[...] * alpha + part
         acc_scr[...] = acc_scr[...] * alpha + jnp.dot(p.astype(jnp.bfloat16), v, preferred_element_type=jnp.float32)
 
-    for far, q_pair in enumerate(((q0, q2), (q1, q3))):
+    @pl.loop(0, 2)
+    def _(far):
+        for side, q_pair in enumerate(((q0, q2), (q1, q3))):
+            @pl.when(far == side)
+            def _():
+                for i in range(2):
+                    for h in range(heads):
+                        n = i * heads + h
+                        q_scr[n * rows:(n + 1) * rows, :] = q_pair[i][:, h * dim:(h + 1) * dim]
+
         t = me ^ (2 * far)
         piece = jnp.where(t < 2, cp, last)
         starts = [piece * 1024 + ((me ^ i) & 1) * 512 + chunk * rows for i in range(2)]
-        for i in range(2):
-            for h in range(heads):
-                n = i * heads + h
-                q_scr[n * rows:(n + 1) * rows, :] = q_pair[i][:, h * dim:(h + 1) * dim]
         m_scr[...] = jnp.full_like(m_scr, -1e30)
         l_scr[...] = jnp.zeros_like(l_scr)
         acc_scr[...] = jnp.zeros_like(acc_scr)
@@ -237,36 +244,53 @@
             step(pl.multiple_of(b * n_keys, n_keys), starts)
 
         out = (acc_scr[...] / jnp.sum(l_scr[...], axis=1, keepdims=True)).astype(jnp.bfloat16)
-        for i, o_ref in enumerate((o_p, o_q)):
+        for i in range(2):
+            row = pl.multiple_of(i * 2 * rows + far * rows, rows)
             for h in range(heads):
                 n = i * heads + h
-                o_ref[far * rows:(far + 1) * rows, h * dim:(h + 1) * dim] = out[n * rows:(n + 1) * rows]
-
-
-def flash(info, qs, sources, chunk, cp_size):
+                o_scr[g, pl.ds(row, rows), h * dim:(h + 1) * dim] = out[n * rows:(n + 1) * rows]
+
+    @pl.when(g == 1)
+    def _():
+        w_copy.wait()
+
+        @pl.loop(0, w_scr.shape[1] // 512)
+        def _(n):
+            cols = pl.ds(pl.multiple_of(n * 512, 512), 512)
+            part = jnp.dot(o_scr[0], w_scr[:heads * dim, cols], preferred_element_type=jnp.float32)
+            part = part + jnp.dot(o_scr[1], w_scr[heads * dim:, cols], preferred_element_type=jnp.float32)
+            part_p[:, cols] = part[:2 * rows].astype(jnp.bfloat16)
+            part_q[:, cols] = part[2 * rows:].astype(jnp.bfloat16)
+
+
+def flash(info, qs, w_o, sources, chunk, cp_size):
     rows = qs[0].shape[0] // N_CHUNKS
     dim = 128
     width = 3 * dim
     seq = cp_size * 2048
     q_spec = pl.BlockSpec((rows, width), lambda g: (chunk, g))
-    o_spec = pl.BlockSpec((2 * rows, width), lambda g: (0, g))
-    o_shape = jax.ShapeDtypeStruct((2 * rows, 2 * width), jnp.bfloat16)
+    model = w_o.shape[1]
+    o_spec = pl.BlockSpec((2 * rows, model), lambda g: (0, 0))
+    o_shape = jax.ShapeDtypeStruct((2 * rows, model), jnp.bfloat16)
     pairs = 4 * rows * seq // 2
     stat = pltpu.VMEM((6 * rows, 128), jnp.float32)
     return pl.pallas_call(
         functools.partial(flash_kernel, rows=rows, chunk=chunk, cp_size=cp_size, dim=dim),
         grid=(2,),
-        in_specs=[pl.BlockSpec(memory_space=pltpu.SMEM)] + [q_spec] * 4 + [pl.BlockSpec(memory_space=pl.ANY)] * len(sources),
+        in_specs=[pl.BlockSpec(memory_space=pltpu.SMEM)] + [q_spec] * 4 + [pl.BlockSpec(memory_space=pl.ANY)] * (1 + len(sources)),
         out_specs=[o_spec, o_spec],
         out_shape=[o_shape, o_shape],
         scratch_shapes=[pltpu.VMEM((2, seq, 2 * dim), jnp.bfloat16),
                         pltpu.VMEM((6 * rows, dim), jnp.bfloat16),
                         stat, stat, stat,
-                        pltpu.SemaphoreType.DMA((2, len(sources)))],
+                        pltpu.VMEM((2, 4 * rows, width), jnp.bfloat16),
+                        pltpu.VMEM(w_o.shape, jnp.bfloat16),
+                        pltpu.SemaphoreType.DMA((2, len(sources))),
+                        pltpu.SemaphoreType.DMA],
         compiler_params=pltpu.CompilerParams(vmem_limit_bytes=60 * 2**20),
         cost_estimate=pl.CostEstimate(flops=8 * pairs * 6 * dim, transcendentals=pairs * 6,
                                       bytes_accessed=seq * 4 * dim * 2),
-    )(info, *qs, *sources)
+    )(info, *qs, w_o, *sources)
 
 
 def solution(mesh):
@@ -334,9 +358,6 @@
         qs = (q_self, q_y, q_core, q_diag)
         sources = tuple(kv_self + kv_y + kv_core + kv_diag)
 
-        def dot(a, b):
-            return jnp.dot(a, b, preferred_element_type=f32)
-
         def after(values, *first):
             return lax.optimization_barrier((values, first))[0]
 
@@ -347,10 +368,9 @@
         mine1, got1, mine2, got2 = {}, {}, {}, {}
 
         def attention(c, *first):
-            o_p, o_q = flash(info, after(qs, *first), sources, c, cp_size)
-            part_q = dot(o_q, w_o).astype(bf16)
+            part_p, part_q = flash(info, after(qs, *first), w_o, sources, c, cp_size)
             got = core_swap(part_q)
-            mine1[c], send = pair_add(dot(after(o_p, part_q), w_o), got)
+            mine1[c], send = pair_add(part_p, got)
             got1[c] = y_swap(send)
             return send
 

time: 718 us -> 718 us (level)
  matrix products: 31.3 us -> 0 us
  Pallas kernels: 276 us -> 298 us
  waiting for transfers between devices: 271 us -> 285 us
  starting transfers between devices: 76 us -> 64.1 us
  local copies, waits for them, and re-layouts: 37.5 us -> 45.2 us
    dot_general x8 -> x0, matrix products: 31.3 us -> none  [dot(): return jnp.dot(a, b, preferred_element_type=f32)]
    pallas_call x4, Pallas kernels: 115 us -> 137 us  [flash(): pl.pallas_call(functools.partial(flash_kernel, rows=rows, chunk=chunk, cp...]
    ppermute x12, starting transfers between devices: 40.7 us -> 29.3 us  [z_gather(): lax.ppermute(right, 'cp', [(i, i + 1) for i in range(hop - 1, cp_size - 1)])]
    ppermute x13, waiting for transfers between devices: 220 us -> 230 us  [y_swap(): return lax.ppermute(v, 'tp', [(t, t ^ 2) for t in range(4)])]
    unnamed x163 -> x155, local copies, waits for them, and re-layouts: 30.2 us -> 37.9 us
  transfers between devices with their start and end apart: 55 -> 55, of which waited for: 18 -> 19; matrix products, arithmetic and copies ran while one was open for 5% -> 3% of each run, Pallas kernels for 22% -> 22%
where the time goes in v2:
time: 718 us; the launch traced here: 708 us
  Pallas kernels  298 us (42%)
  waiting for transfers between devices  285 us (40%)
  starting transfers between devices  64.1 us (9%)
  local copies, waits for them, and re-layouts  45.2 us (6%)
  other arithmetic  14.4 us (2%)
    ppermute x13, waiting for transfers between devices, y_swap(): return lax.ppermute(v, 'tp', [(t, t ^ 2) for t in range(4)])  230 us
    pallas_call x4, Pallas kernels, flash(): pl.pallas_call(functools.partial(flash_kernel, rows=rows, chunk=chunk, cp...  137 us
    pallas_call x2, Pallas kernels, gate_up(): pl.pallas_call(gate_up_kernel, grid=(hidden // block,), in_specs=[piece]...  65.1 us
    pallas_call x3, Pallas kernels, down(): pl.pallas_call(down_kernel, grid=(width // block,), in_specs=[pl.BlockSpe...  41.5 us
    pallas_call x8, Pallas kernels, project(): pl.pallas_call(functools.partial(proj_kernel, rope_heads=rope_heads), gri...  40.5 us
    ppermute x12, waiting for transfers between devices, z_gather(): lax.ppermute(left, 'cp', [(i, i - 1) for i in range(1, cp_size - hop + 1)])  40.3 us
    unnamed x155, local copies, waits for them, and re-layouts  37.9 us
    ppermute x12, starting transfers between devices, z_gather(): lax.ppermute(right, 'cp', [(i, i + 1) for i in range(hop - 1, cp_size - 1)])  29.3 us
  transfers between devices with their start and end apart: 55, of which 19 were waited for; matrix products, arithmetic and copies ran while one was open for 3% of the time, Pallas kernels for 22%

profile of v2, /device:TPU:0, one launch (start us, length us, event | category | flops | bytes accessed | tf_op | source)
XLA Modules:
  0.0 707.6 jit_solution(17884282401177639327)
XLA Ops:
  9.4 68.4 %collective-permute-done.a_ref = bf16[512,3072]{1,0:T(8,128)(2,1)} collective-permute-done((bf16[512,3072]{1,0:T(8,128)(2,1)}, bf16[512,3072]{1,0:T(8,128)(2,1)}, u32[]{:S(2)}, u32[]{:S(2)}) %collective-permute-start) | collective-permute-done | bytes 3145760 | tf_op jit(solution)/shard_map/ppermute | solution.py:306
  92.0 10.5 %collective-permute-done.3.rest_2_ = bf16[512,512]{1,0:T(8,128)(2,1)S(1)} collective-permute-done((bf16[512,512]{1,0:T(8,128)(2,1)S(1)}, bf16[512,512]{1,0:T(8,128)(2,1)S(1)}, u32[]{:S(2)}, u32[]{:S(2)}) %collective-permute-start.3) | collective-permute-done | bytes 524320 | tf_op jit(solution)/shard_map/ppermute | solution.py:312
  109.1 12.7 %collective-permute-done.7.rest_5_ = bf16[512,512]{1,0:T(8,128)(2,1)S(1)} collective-permute-done((bf16[512,512]{1,0:T(8,128)(2,1)S(1)}, bf16[512,512]{1,0:T(8,128)(2,1)S(1)}, u32[]{:S(2)}, u32[]{:S(2)}) %collective-permute-start.7) | collective-permute-done | bytes 524320 | tf_op jit(solution)/shard_map/ppermute | solution.py:313
  137.8 5.5 collective-permute-start.15
  152.1 6.7 collective-permute-start.21
  167.6 8.4 %collective-permute-done.13.rest_12_ = bf16[512,512]{1,0:T(8,128)(2,1)S(1)} collective-permute-done((bf16[512,512]{1,0:T(8,128)(2,1)S(1)}, bf16[512,512]{1,0:T(8,128)(2,1)S(1)}, u32[]{:S(2)}, u32[]{:S(2)}) %collective-permute-start.13) | collective-permute-done | bytes 524320 | tf_op jit(solution)/shard_map/ppermute | solution.py:313
  178.9 8.4 %collective-permute-done.24.rest_25_ = bf16[512,512]{1,0:T(8,128)(2,1)} collective-permute-done((bf16[512,512]{1,0:T(8,128)(2,1)S(1)}, bf16[512,512]{1,0:T(8,128)(2,1)}, u32[]{:S(2)}, u32[]{:S(2)}) %collective-permute-start.24) | collective-permute-done | bytes 524320 | tf_op jit(solution)/shard_map/ppermute | solution.py:313
  188.6 6.7 copy.12
  195.3 6.6 copy.13.w0_ref.w1_ref
  206.9 5.9 shard_map.100.q0
  219.2 5.8 shard_map.101.q1
  225.8 5.8 shard_map.102.q2
  232.5 5.7 shard_map.103.q3
  246.0 34.2 %shard_map.108 = (bf16[256,3072]{1,0:T(8,128)(2,1)}, bf16[256,3072]{1,0:T(8,128)(2,1)}) custom-call(s32[2]{0:T(128)} %pad_add_fusion.info_ref, bf16[512,768]{1,0:T(8,128)(2,1)} %copy-done.39, bf16[512,768]{1,0:T(8,128)(2,1)} %copy-done.40, bf16[512,768]{1,0:T(8,128)(2,1)} %copy-done.41, bf16[512,768]{1,0:T(8,128)(2,1)} %copy-done.42, ...), custom_call_target="tpu_custom_call" | custom-call | flops 12884901888 | bytes 8388608 | tf_op jit(solution)/shard_map/pallas_call | solution.py:277
  288.2 34.6 %shard_map.111 = (bf16[256,3072]{1,0:T(8,128)(2,1)}, bf16[256,3072]{1,0:T(8,128)(2,1)}) custom-call(s32[2]{0:T(128)} %pad_add_fusion.info_ref, bf16[512,768]{1,0:T(8,128)(2,1)} %copy-done.39, bf16[512,768]{1,0:T(8,128)(2,1)} %copy-done.40, bf16[512,768]{1,0:T(8,128)(2,1)} %copy-done.41, bf16[512,768]{1,0:T(8,128)(2,1)} %copy-done.42, ...), custom_call_target="tpu_custom_call" | custom-call | flops 12884901888 | bytes 8388608 | tf_op jit(solution)/shard_map/pallas_call | solution.py:277
  324.6 18.5 %collective-permute-done.28.got_ref = bf16[128,3072]{1,0:T(8,128)(2,1)S(1)} collective-permute-done((bf16[128,3072]{1,0:T(8,128)(2,1)}, bf16[128,3072]{1,0:T(8,128)(2,1)S(1)}, u32[]{:S(2)}, u32[]{:S(2)}) %collective-permute-start.28) | collective-permute-done | bytes 786464 | tf_op jit(solution)/shard_map/ppermute | solution.py:306
  349.7 34.2 %shard_map.114 = (bf16[256,3072]{1,0:T(8,128)(2,1)}, bf16[256,3072]{1,0:T(8,128)(2,1)}) custom-call(s32[2]{0:T(128)} %pad_add_fusion.info_ref, bf16[512,768]{1,0:T(8,128)(2,1)} %copy-done.39, bf16[512,768]{1,0:T(8,128)(2,1)} %copy-done.40, bf16[512,768]{1,0:T(8,128)(2,1)} %copy-done.41, bf16[512,768]{1,0:T(8,128)(2,1)} %copy-done.42, ...), custom_call_target="tpu_custom_call" | custom-call | flops 12884901888 | bytes 8388608 | tf_op jit(solution)/shard_map/pallas_call | solution.py:277
  385.6 18.6 %collective-permute-done.33.got_ref = bf16[128,3072]{1,0:T(8,128)(2,1)S(1)} collective-permute-done((bf16[128,3072]{1,0:T(8,128)(2,1)}, bf16[128,3072]{1,0:T(8,128)(2,1)S(1)}, u32[]{:S(2)}, u32[]{:S(2)}) %collective-permute-start.33) | collective-permute-done | bytes 786464 | tf_op jit(solution)/shard_map/ppermute | solution.py:306
  410.8 34.3 %shard_map.116 = (bf16[256,3072]{1,0:T(8,128)(2,1)}, bf16[256,3072]{1,0:T(8,128)(2,1)}) custom-call(s32[2]{0:T(128)} %pad_add_fusion.info_ref, bf16[512,768]{1,0:T(8,128)(2,1)} %copy-done.39, bf16[512,768]{1,0:T(8,128)(2,1)} %copy-done.40, bf16[512,768]{1,0:T(8,128)(2,1)} %copy-done.41, bf16[512,768]{1,0:T(8,128)(2,1)} %copy-done.42, ...), custom_call_target="tpu_custom_call" | custom-call | flops 12884901888 | bytes 8388608 | tf_op jit(solution)/shard_map/pallas_call | solution.py:277
  448.8 17.1 %collective-permute-done.29.refs_1_ = bf16[128,3072]{1,0:T(8,128)(2,1)S(1)} collective-permute-done((bf16[128,3072]{1,0:T(8,128)(2,1)}, bf16[128,3072]{1,0:T(8,128)(2,1)S(1)}, u32[]{:S(2)}, u32[]{:S(2)}) %collective-permute-start.29) | collective-permute-done | bytes 786464 | tf_op jit(solution)/shard_map/ppermute | solution.py:306
  465.9 16.8 %collective-permute-done.34.refs_5_ = bf16[128,3072]{1,0:T(8,128)(2,1)S(1)} collective-permute-done((bf16[128,3072]{1,0:T(8,128)(2,1)}, bf16[128,3072]{1,0:T(8,128)(2,1)S(1)}, u32[]{:S(2)}, u32[]{:S(2)}) %collective-permute-start.34) | collective-permute-done | bytes 786464 | tf_op jit(solution)/shard_map/ppermute | solution.py:306
  485.6 13.4 %collective-permute-done.39.got_ref = bf16[128,3072]{1,0:T(8,128)(2,1)S(1)} collective-permute-done((bf16[128,3072]{1,0:T(8,128)(2,1)}, bf16[128,3072]{1,0:T(8,128)(2,1)S(1)}, u32[]{:S(2)}, u32[]{:S(2)}) %collective-permute-start.39) | collective-permute-done | bytes 786464 | tf_op jit(solution)/shard_map/ppermute | solution.py:306
  502.6 16.9 %collective-permute-done.47.got_ref = bf16[128,3072]{1,0:T(8,128)(2,1)S(1)} collective-permute-done((bf16[128,3072]{1,0:T(8,128)(2,1)S(1)}, bf16[128,3072]{1,0:T(8,128)(2,1)S(1)}, u32[]{:S(2)}, u32[]{:S(2)}) %collective-permute-start.47) | collective-permute-done | bytes 786464 | tf_op jit(solution)/shard_map/ppermute | solution.py:306
  523.5 32.5 %shard_map.119.u_ref = bf16[1024,2048]{1,0:T(8,128)(2,1)} custom-call(bf16[128,3072]{1,0:T(8,128)(2,1)} %copy-done.47, bf16[128,3072]{1,0:T(8,128)(2,1)} %copy-done.55, bf16[128,3072]{1,0:T(8,128)(2,1)} %copy-done.57, bf16[128,3072]{1,0:T(8,128)(2,1)} %copy-done.58, bf16[128,3072]{1,0:T(8,128)(2,1)} %copy-done.48, bf16[128,3072]{1,0:T(8,128)(2,1)} %copy-done.56, ...), custom_call_target="tpu_custom_call" | custom-call | flops 25769803776 | bytes 35651584 | tf_op jit(solution)/shard_map/pallas_call | solution.py:122
  556.7 18.1 %shard_map.120 = (bf16[256,3072]{1,0:T(8,128)(2,1)}, bf16[256,3072]{1,0:T(8,128)(2,1)}, bf16[256,3072]{1,0:T(8,128)(2,1)}, bf16[256,3072]{1,0:T(8,128)(2,1)}) custom-call(bf16[1024,2048]{1,0:T(8,128)(2,1)} %shard_map.119.u_ref, bf16[2048,3072]{1,0:T(8,128)(2,1)} %w_ref.5), custom_call_target="tpu_custom_call" | custom-call | flops 12884901888 | bytes 23068672 | tf_op jit(solution)/shard_map/pallas_call | solution.py:149
  575.3 32.6 %shard_map.124.u_ref = bf16[1024,2048]{1,0:T(8,128)(2,1)} custom-call(bf16[128,3072]{1,0:T(8,128)(2,1)} %get-tuple-element.132.refs_0_, bf16[128,3072]{1,0:T(8,128)(2,1)} %collective-permute-done.44.refs_1_, bf16[128,3072]{1,0:T(8,128)(2,1)} %collective-permute-done.45.refs_2_, bf16[128,3072]{1,0:T(8,128)(2,1)} %collective-permute-done.46.refs_3_, ...), custom_call_target="tpu_custom_call" | custom-call | flops 25769803776 | bytes 35651584 | tf_op jit(solution)/shard_map/pallas_call | solution.py:122
  607.9 11.7 %shard_map.127 = (bf16[256,3072]{1,0:T(8,128)(2,1)}, bf16[256,3072]{1,0:T(8,128)(2,1)}) custom-call(bf16[1024,2048]{1,0:T(8,128)(2,1)} %shard_map.124.u_ref, bf16[2048,3072]{1,0:T(8,128)(2,1)} %w_ref.5), custom_call_target="tpu_custom_call" | custom-call | flops 6442450944 | bytes 17825792 | tf_op jit(solution)/shard_map/pallas_call | solution.py:149
  619.8 11.7 %shard_map.125 = (bf16[256,3072]{1,0:T(8,128)(2,1)}, bf16[256,3072]{1,0:T(8,128)(2,1)}) custom-call(bf16[1024,2048]{1,0:T(8,128)(2,1)} %shard_map.124.u_ref, bf16[2048,3072]{1,0:T(8,128)(2,1)} %w_ref.5), custom_call_target="tpu_custom_call" | custom-call | flops 6442450944 | bytes 17825792 | tf_op jit(solution)/shard_map/pallas_call | solution.py:149
  641.4 14.1 %collective-permute-done.43 = bf16[128,3072]{1,0:T(8,128)(2,1)S(1)} collective-permute-done((bf16[128,3072]{1,0:T(8,128)(2,1)S(1)}, bf16[128,3072]{1,0:T(8,128)(2,1)S(1)}, u32[]{:S(2)}, u32[]{:S(2)}) %collective-permute-start.43) | collective-permute-done | bytes 786464 | tf_op jit(solution)/shard_map/ppermute | solution.py:306
  658.2 14.1 %collective-permute-done.41 = bf16[128,3072]{1,0:T(8,128)(2,1)S(1)} collective-permute-done((bf16[128,3072]{1,0:T(8,128)(2,1)S(1)}, bf16[128,3072]{1,0:T(8,128)(2,1)S(1)}, u32[]{:S(2)}, u32[]{:S(2)}) %collective-permute-start.41) | collective-permute-done | bytes 786464 | tf_op jit(solution)/shard_map/ppermute | solution.py:306
  672.7 16.6 %collective-permute-done.54 = bf16[128,3072]{1,0:T(8,128)(2,1)S(1)} collective-permute-done((bf16[128,3072]{1,0:T(8,128)(2,1)S(1)}, bf16[128,3072]{1,0:T(8,128)(2,1)S(1)}, u32[]{:S(2)}, u32[]{:S(2)}) %collective-permute-start.54) | collective-permute-done | bytes 786464 | tf_op jit(solution)/shard_map/ppermute | solution.py:306
  689.5 15.8 %collective-permute-done.52 = bf16[128,3072]{1,0:T(8,128)(2,1)S(1)} collective-permute-done((bf16[128,3072]{1,0:T(8,128)(2,1)S(1)}, bf16[128,3072]{1,0:T(8,128)(2,1)S(1)}, u32[]{:S(2)}, u32[]{:S(2)}) %collective-permute-start.52) | collective-permute-done | bytes 786464 | tf_op jit(solution)/shard_map/ppermute | solution.py:306
  (285 shorter events, 143.4 us)
Async XLA Ops:
  6.4 71.4 %collective-permute-start = (bf16[512,3072]{1,0:T(8,128)(2,1)}, bf16[512,3072]{1,0:T(8,128)(2,1)}, u32[]{:S(2)}, u32[]{:S(2)}) collective-permute-start(bf16[512,3072]{1,0:T(8,128)(2,1)} %fusion.2.a_ref), channel_id=1, source_target_pairs={{0,2},{1,3},{2,0},{3,1},{4,6},{5,7},{6,4},{7,5},{8,10},{9,11},{10,... | collective-permute-start | bytes 9437192 | tf_op jit(solution)/shard_map/ppermute | solution.py:306
  9.4 122.8 %collective-permute-start.1 = (bf16[512,3072]{1,0:T(8,128)(2,1)}, bf16[512,3072]{1,0:T(8,128)(2,1)}, u32[]{:S(2)}, u32[]{:S(2)}) collective-permute-start(bf16[512,3072]{1,0:T(8,128)(2,1)} %fusion.2.a_ref), channel_id=1, source_target_pairs={{0,1},{1,0},{2,3},{3,2},{4,5},{5,4},{6,7},{7,6},{8,9},{9,8},{10,11... | collective-permute-start | bytes 9437192 | tf_op jit(solution)/shard_map/ppermute | solution.py:303
  77.8 60.0 %collective-permute-start.2 = (bf16[512,3072]{1,0:T(8,128)(2,1)}, bf16[512,3072]{1,0:T(8,128)(2,1)}, u32[]{:S(2)}, u32[]{:S(2)}) collective-permute-start(bf16[512,3072]{1,0:T(8,128)(2,1)} %collective-permute-done.a_ref), channel_id=1, source_target_pairs={{0,1},{1,0},{2,3},{3,2},{4,5},{5,4},{6,7},{7,6},{8,9},{9,8},{10,11... | collective-permute-start | bytes 9437192 | tf_op jit(solution)/shard_map/ppermute | solution.py:303
  108.4 39.6 %collective-permute-start.5 = (bf16[512,512]{1,0:T(8,128)(2,1)S(1)}, bf16[512,512]{1,0:T(8,128)(2,1)S(1)}, u32[]{:S(2)}, u32[]{:S(2)}) collective-permute-start(bf16[512,512]{1,0:T(8,128)(2,1)S(1)} %collective-permute-done.4.rest_1_), channel_id=1, source_target_pairs={{8,12},{9,13},{10,14},{11,15},{24,28},{25,29},{26,30},{27,31}} | collective-permute-start | bytes 1572872 | tf_op jit(solution)/shard_map/ppermute | solution.py:312
  121.8 30.3 %collective-permute-start.8 = (bf16[512,512]{1,0:T(8,128)(2,1)S(1)}, bf16[512,512]{1,0:T(8,128)(2,1)S(1)}, u32[]{:S(2)}, u32[]{:S(2)}) collective-permute-start(bf16[512,512]{1,0:T(8,128)(2,1)S(1)} %collective-permute-done.7.rest_5_), channel_id=1, source_target_pairs={{4,0},{5,1},{6,2},{7,3},{20,16},{21,17},{22,18},{23,19}} | collective-permute-start | bytes 1572872 | tf_op jit(solution)/shard_map/ppermute | solution.py:313
  150.8 25.1 %collective-permute-start.13 = (bf16[512,512]{1,0:T(8,128)(2,1)S(1)}, bf16[512,512]{1,0:T(8,128)(2,1)S(1)}, u32[]{:S(2)}, u32[]{:S(2)}) collective-permute-start(bf16[512,512]{1,0:T(8,128)(2,1)S(1)} %collective-permute-done.12.rest_11_), channel_id=1, source_target_pairs={{4,0},{8,4},{5,1},{9,5},{6,2},{10,6},{7,3},{11,7},{20,16},{24,20},... | collective-permute-start | bytes 1572872 | tf_op jit(solution)/shard_map/ppermute | solution.py:313
  152.1 25.3 %collective-permute-start.21 = (bf16[512,512]{1,0:T(8,128)(2,1)S(1)}, bf16[512,512]{1,0:T(8,128)(2,1)}, u32[]{:S(2)}, u32[]{:S(2)}) collective-permute-start(bf16[512,512]{1,0:T(8,128)(2,1)S(1)} %shard_map.107.rest_24_), channel_id=1, source_target_pairs={{0,4},{4,8},{8,12},{1,5},{5,9},{9,13},{2,6},{6,10},{10,14},{3,7},{... | collective-permute-start | bytes 1572872 | tf_op jit(solution)/shard_map/ppermute | solution.py:312
  158.9 28.4 %collective-permute-start.24 = (bf16[512,512]{1,0:T(8,128)(2,1)S(1)}, bf16[512,512]{1,0:T(8,128)(2,1)}, u32[]{:S(2)}, u32[]{:S(2)}) collective-permute-start(bf16[512,512]{1,0:T(8,128)(2,1)S(1)} %shard_map.107.rest_24_), channel_id=1, source_target_pairs={{4,0},{8,4},{12,8},{5,1},{9,5},{13,9},{6,2},{10,6},{14,10},{7,3},{... | collective-permute-start | bytes 1572872 | tf_op jit(solution)/shard_map/ppermute | solution.py:313
  164.8 48.9 %collective-permute-start.16 = (bf16[512,512]{1,0:T(8,128)(2,1)}, bf16[512,512]{1,0:T(8,128)(2,1)}, u32[]{:S(2)}, u32[]{:S(2)}) collective-permute-start(bf16[512,512]{1,0:T(8,128)(2,1)} %collective-permute-done.15.rest_16_), channel_id=1, source_target_pairs={{4,8},{8,12},{5,9},{9,13},{6,10},{10,14},{7,11},{11,15},{20,24},{2... | collective-permute-start | bytes 1572872 | tf_op jit(solution)/shard_map/ppermute | solution.py:312
  166.3 48.8 %collective-permute-start.19 = (bf16[512,512]{1,0:T(8,128)(2,1)}, bf16[512,512]{1,0:T(8,128)(2,1)}, u32[]{:S(2)}, u32[]{:S(2)}) collective-permute-start(bf16[512,512]{1,0:T(8,128)(2,1)} %collective-permute-done.18.rest_18_), channel_id=1, source_target_pairs={{4,0},{8,4},{5,1},{9,5},{6,2},{10,6},{7,3},{11,7},{20,16},{24,20},... | collective-permute-start | bytes 1572872 | tf_op jit(solution)/shard_map/ppermute | solution.py:313
  175.9 39.9 %collective-permute-start.11 = (bf16[512,512]{1,0:T(8,128)(2,1)}, bf16[512,512]{1,0:T(8,128)(2,1)}, u32[]{:S(2)}, u32[]{:S(2)}) collective-permute-start(bf16[512,512]{1,0:T(8,128)(2,1)} %collective-permute-done.10.rest_8_), channel_id=1, source_target_pairs={{8,12},{9,13},{10,14},{11,15},{24,28},{25,29},{26,30},{27,31}} | collective-permute-start | bytes 1572872 | tf_op jit(solution)/shard_map/ppermute | solution.py:312
  177.5 39.7 %collective-permute-start.22 = (bf16[512,512]{1,0:T(8,128)(2,1)}, bf16[512,512]{1,0:T(8,128)(2,1)}, u32[]{:S(2)}, u32[]{:S(2)}) collective-permute-start(bf16[512,512]{1,0:T(8,128)(2,1)} %collective-permute-done.21.rest_23_), channel_id=1, source_target_pairs={{4,8},{8,12},{5,9},{9,13},{6,10},{10,14},{7,11},{11,15},{20,24},{2... | collective-permute-start | bytes 1572872 | tf_op jit(solution)/shard_map/ppermute | solution.py:312
  187.3 30.5 %collective-permute-start.25 = (bf16[512,512]{1,0:T(8,128)(2,1)}, bf16[512,512]{1,0:T(8,128)(2,1)}, u32[]{:S(2)}, u32[]{:S(2)}) collective-permute-start(bf16[512,512]{1,0:T(8,128)(2,1)} %collective-permute-done.24.rest_25_), channel_id=1, source_target_pairs={{4,0},{8,4},{5,1},{9,5},{6,2},{10,6},{7,3},{11,7},{20,16},{24,20},... | collective-permute-start | bytes 1572872 | tf_op jit(solution)/shard_map/ppermute | solution.py:313
  213.7 25.5 %collective-permute-start.14 = (bf16[512,512]{1,0:T(8,128)(2,1)S(1)}, bf16[512,512]{1,0:T(8,128)(2,1)S(1)}, u32[]{:S(2)}, u32[]{:S(2)}) collective-permute-start(bf16[512,512]{1,0:T(8,128)(2,1)S(1)} %copy-done.71), channel_id=1, source_target_pairs={{4,0},{5,1},{6,2},{7,3},{20,16},{21,17},{22,18},{23,19}} | collective-permute-start | bytes 1572872 | tf_op jit(solution)/shard_map/ppermute | solution.py:313
  215.1 24.9 %collective-permute-start.17 = (bf16[512,512]{1,0:T(8,128)(2,1)}, bf16[512,512]{1,0:T(8,128)(2,1)S(1)}, u32[]{:S(2)}, u32[]{:S(2)}) collective-permute-start(bf16[512,512]{1,0:T(8,128)(2,1)} %collective-permute-done.16.rest_15_), channel_id=1, source_target_pairs={{8,12},{9,13},{10,14},{11,15},{24,28},{25,29},{26,30},{27,31}} | collective-permute-start | bytes 1572872 | tf_op jit(solution)/shard_map/ppermute | solution.py:312
  215.8 25.0 %collective-permute-start.20 = (bf16[512,512]{1,0:T(8,128)(2,1)}, bf16[512,512]{1,0:T(8,128)(2,1)S(1)}, u32[]{:S(2)}, u32[]{:S(2)}) collective-permute-start(bf16[512,512]{1,0:T(8,128)(2,1)} %collective-permute-done.19.rest_19_), channel_id=1, source_target_pairs={{4,0},{5,1},{6,2},{7,3},{20,16},{21,17},{22,18},{23,19}} | collective-permute-start | bytes 1572872 | tf_op jit(solution)/shard_map/ppermute | solution.py:313
  217.1 24.5 %collective-permute-start.23 = (bf16[512,512]{1,0:T(8,128)(2,1)}, bf16[512,512]{1,0:T(8,128)(2,1)S(1)}, u32[]{:S(2)}, u32[]{:S(2)}) collective-permute-start(bf16[512,512]{1,0:T(8,128)(2,1)} %collective-permute-done.22.rest_22_), channel_id=1, source_target_pairs={{8,12},{9,13},{10,14},{11,15},{24,28},{25,29},{26,30},{27,31}} | collective-permute-start | bytes 1572872 | tf_op jit(solution)/shard_map/ppermute | solution.py:312
  217.9 27.3 %collective-permute-start.26 = (bf16[512,512]{1,0:T(8,128)(2,1)}, bf16[512,512]{1,0:T(8,128)(2,1)S(1)}, u32[]{:S(2)}, u32[]{:S(2)}) collective-permute-start(bf16[512,512]{1,0:T(8,128)(2,1)} %collective-permute-done.25.rest_26_), channel_id=1, source_target_pairs={{4,0},{5,1},{6,2},{7,3},{20,16},{21,17},{22,18},{23,19}} | collective-permute-start | bytes 1572872 | tf_op jit(solution)/shard_map/ppermute | solution.py:313
  445.1 37.6 %collective-permute-start.38 = (bf16[256,3072]{1,0:T(8,128)(2,1)}, bf16[256,3072]{1,0:T(8,128)(2,1)S(1)}, u32[]{:S(2)}, u32[]{:S(2)}) collective-permute-start(bf16[256,3072]{1,0:T(8,128)(2,1)} %get-tuple-element.108), channel_id=1, source_target_pairs={{0,1},{1,0},{2,3},{3,2},{4,5},{5,4},{6,7},{7,6},{8,9},{9,8},{10,11... | collective-permute-start | bytes 4718600 | tf_op jit(solution)/shard_map/ppermute | solution.py:303
  446.8 35.9 %collective-permute-start.34 = (bf16[128,3072]{1,0:T(8,128)(2,1)}, bf16[128,3072]{1,0:T(8,128)(2,1)S(1)}, u32[]{:S(2)}, u32[]{:S(2)}) collective-permute-start(bf16[128,3072]{1,0:T(8,128)(2,1)} %copy-done.48), channel_id=1, source_target_pairs={{0,2},{1,3},{2,0},{3,1},{4,6},{5,7},{6,4},{7,5},{8,10},{9,11},{10,... | collective-permute-start | bytes 2359304 | tf_op jit(solution)/shard_map/ppermute | solution.py:306
  447.3 51.8 %collective-permute-start.39 = (bf16[128,3072]{1,0:T(8,128)(2,1)}, bf16[128,3072]{1,0:T(8,128)(2,1)S(1)}, u32[]{:S(2)}, u32[]{:S(2)}) collective-permute-start(bf16[128,3072]{1,0:T(8,128)(2,1)} %copy-done.49), channel_id=1, source_target_pairs={{0,2},{1,3},{2,0},{3,1},{4,6},{5,7},{6,4},{7,5},{8,10},{9,11},{10,... | collective-permute-start | bytes 2359304 | tf_op jit(solution)/shard_map/ppermute | solution.py:306
  448.8 53.2 %collective-permute-start.30 = (bf16[128,3072]{1,0:T(8,128)(2,1)}, bf16[128,3072]{1,0:T(8,128)(2,1)S(1)}, u32[]{:S(2)}, u32[]{:S(2)}) collective-permute-start(bf16[128,3072]{1,0:T(8,128)(2,1)} %copy-done.47), channel_id=1, source_target_pairs={{0,1},{1,0},{2,3},{3,2},{4,5},{5,4},{6,7},{7,6},{8,9},{9,8},{10,11... | collective-permute-start | bytes 2359304 | tf_op jit(solution)/shard_map/ppermute | solution.py:303
  465.9 36.7 %collective-permute-start.31 = (bf16[128,3072]{1,0:T(8,128)(2,1)S(1)}, bf16[128,3072]{1,0:T(8,128)(2,1)S(1)}, u32[]{:S(2)}, u32[]{:S(2)}) collective-permute-start(bf16[128,3072]{1,0:T(8,128)(2,1)S(1)} %collective-permute-done.29.refs_1_), channel_id=1, source_target_pairs={{0,1},{1,0},{2,3},{3,2},{4,5},{5,4},{6,7},{7,6},{8,9},{9,8},{10,11... | collective-permute-start | bytes 2359304 | tf_op jit(solution)/shard_map/ppermute | solution.py:303
  502.1 54.0 %collective-permute-start.44 = (bf16[128,3072]{1,0:T(8,128)(2,1)}, bf16[128,3072]{1,0:T(8,128)(2,1)}, u32[]{:S(2)}, u32[]{:S(2)}) collective-permute-start(bf16[128,3072]{1,0:T(8,128)(2,1)} %get-tuple-element.132.refs_0_), channel_id=1, source_target_pairs={{0,2},{1,3},{2,0},{3,1},{4,6},{5,7},{6,4},{7,5},{8,10},{9,11},{10,... | collective-permute-start | bytes 2359304 | tf_op jit(solution)/shard_map/ppermute | solution.py:306
  502.6 72.4 %collective-permute-start.45 = (bf16[128,3072]{1,0:T(8,128)(2,1)}, bf16[128,3072]{1,0:T(8,128)(2,1)}, u32[]{:S(2)}, u32[]{:S(2)}) collective-permute-start(bf16[128,3072]{1,0:T(8,128)(2,1)} %get-tuple-element.132.refs_0_), channel_id=1, source_target_pairs={{0,1},{1,0},{2,3},{3,2},{4,5},{5,4},{6,7},{7,6},{8,9},{9,8},{10,11... | collective-permute-start | bytes 2359304 | tf_op jit(solution)/shard_map/ppermute | solution.py:303
  522.0 34.7 %collective-permute-start.48 = (bf16[128,3072]{1,0:T(8,128)(2,1)}, bf16[128,3072]{1,0:T(8,128)(2,1)S(1)}, u32[]{:S(2)}, u32[]{:S(2)}) collective-permute-start(bf16[128,3072]{1,0:T(8,128)(2,1)} %get-tuple-element.136.refs_4_), channel_id=1, source_target_pairs={{0,2},{1,3},{2,0},{3,1},{4,6},{5,7},{6,4},{7,5},{8,10},{9,11},{10,... | collective-permute-start | bytes 2359304 | tf_op jit(solution)/shard_map/ppermute | solution.py:306
  574.8 57.0 %collective-permute-start.42 = (bf16[256,3072]{1,0:T(8,128)(2,1)}, bf16[256,3072]{1,0:T(8,128)(2,1)}, u32[]{:S(2)}, u32[]{:S(2)}) collective-permute-start(bf16[256,3072]{1,0:T(8,128)(2,1)} %get-tuple-element.126), channel_id=1, source_target_pairs={{0,1},{1,0},{2,3},{3,2},{4,5},{5,4},{6,7},{7,6},{8,9},{9,8},{10,11... | collective-permute-start | bytes 4718600 | tf_op jit(solution)/shard_map/ppermute | solution.py:303
  575.0 60.6 %collective-permute-start.40 = (bf16[256,3072]{1,0:T(8,128)(2,1)}, bf16[256,3072]{1,0:T(8,128)(2,1)}, u32[]{:S(2)}, u32[]{:S(2)}) collective-permute-start(bf16[256,3072]{1,0:T(8,128)(2,1)} %get-tuple-element.121), channel_id=1, source_target_pairs={{0,1},{1,0},{2,3},{3,2},{4,5},{5,4},{6,7},{7,6},{8,9},{9,8},{10,11... | collective-permute-start | bytes 4718600 | tf_op jit(solution)/shard_map/ppermute | solution.py:303
  631.5 24.3 %collective-permute-start.51 = (bf16[256,3072]{1,0:T(8,128)(2,1)}, bf16[256,3072]{1,0:T(8,128)(2,1)S(1)}, u32[]{:S(2)}, u32[]{:S(2)}) collective-permute-start(bf16[256,3072]{1,0:T(8,128)(2,1)} %get-tuple-element.141), channel_id=1, source_target_pairs={{0,1},{1,0},{2,3},{3,2},{4,5},{5,4},{6,7},{7,6},{8,9},{9,8},{10,11... | collective-permute-start | bytes 4718600 | tf_op jit(solution)/shard_map/ppermute | solution.py:303
  637.4 34.9 %collective-permute-start.41 = (bf16[128,3072]{1,0:T(8,128)(2,1)S(1)}, bf16[128,3072]{1,0:T(8,128)(2,1)S(1)}, u32[]{:S(2)}, u32[]{:S(2)}) collective-permute-start(bf16[128,3072]{1,0:T(8,128)(2,1)S(1)} %get-tuple-element.123), channel_id=1, source_target_pairs={{0,2},{1,3},{2,0},{3,1},{4,6},{5,7},{6,4},{7,5},{8,10},{9,11},{10,... | collective-permute-start | bytes 2359304 | tf_op jit(solution)/shard_map/ppermute | solution.py:306
  640.8 48.4 %collective-permute-start.54 = (bf16[128,3072]{1,0:T(8,128)(2,1)S(1)}, bf16[128,3072]{1,0:T(8,128)(2,1)S(1)}, u32[]{:S(2)}, u32[]{:S(2)}) collective-permute-start(bf16[128,3072]{1,0:T(8,128)(2,1)S(1)} %get-tuple-element.148), channel_id=1, source_target_pairs={{0,2},{1,3},{2,0},{3,1},{4,6},{5,7},{6,4},{7,5},{8,10},{9,11},{10,... | collective-permute-start | bytes 2359304 | tf_op jit(solution)/shard_map/ppermute | solution.py:306
  657.7 47.7 %collective-permute-start.52 = (bf16[128,3072]{1,0:T(8,128)(2,1)S(1)}, bf16[128,3072]{1,0:T(8,128)(2,1)S(1)}, u32[]{:S(2)}, u32[]{:S(2)}) collective-permute-start(bf16[128,3072]{1,0:T(8,128)(2,1)S(1)} %get-tuple-element.143), channel_id=1, source_target_pairs={{0,2},{1,3},{2,0},{3,1},{4,6},{5,7},{6,4},{7,5},{8,10},{9,11},{10,... | collective-permute-start | bytes 2359304 | tf_op jit(solution)/shard_map/ppermute | solution.py:306
  (100 other events, 1153.0 us)
